TPU v7x, 32 devices: a whole 2x2x4 slice. The times are simulated.
32 devices in a mesh: batch: 4 (over z), rows: 8 (over y, x, core).
Axes of the slice: x: 2, y: 2, z: 4, core: 2. Of those that a mesh axis runs over, the one named last changes fastest.
Arguments:
- level_two: bfloat16 [8, 64, 256, 256], P('batch', 'rows'), parts along dimension 0, may hold values from -130 to 130
- level_three: bfloat16 [8, 32, 128, 512], P('batch', 'rows'), parts along dimension 0, may hold values from -130 to 130
- level_four: bfloat16 [8, 16, 64, 1024], P('batch', 'rows'), parts along dimension 0, may hold values from -130 to 130
- level_five: bfloat16 [8, 8, 32, 2048], P('batch', 'rows'), parts along dimension 0, may hold values from -130 to 130
- lateral_two: bfloat16 [256, 256], replicated, may hold values from -0.375 to 0.375
- lateral_three: bfloat16 [512, 256], replicated, may hold values from -0.25 to 0.25
- lateral_four: bfloat16 [1024, 256], replicated, may hold values from -0.1875 to 0.1875
- lateral_five: bfloat16 [2048, 256], replicated, may hold values from -0.125 to 0.125
- lateral_bias: float32 [4, 256], replicated, may hold values from -4 to 4
- smooth_weight: bfloat16 [4, 3, 768, 256], replicated, may hold values from -0.125 to 0.125
- norm_gain: float32 [4, 256], replicated, may hold values from 0.5 to 1.5
- norm_shift: float32 [4, 256], replicated, may hold values from -2 to 2
Outputs:
- pyramid_two: bfloat16 [8, 64, 256, 256], P('batch', 'rows'), parts along dimension 0
- pyramid_three: bfloat16 [8, 32, 128, 256], P('batch', 'rows'), parts along dimension 0
- pyramid_four: bfloat16 [8, 16, 64, 256], P('batch', 'rows'), parts along dimension 0
- pyramid_five: bfloat16 [8, 8, 32, 256], P('batch', 'rows'), parts along dimension 0
There are 4 independent parts, one for each index of `batch`. A program takes and returns all parts, laid end to end along the dimension named above; an argument that names none is the same for every part. Nothing has to cross between parts.
All inputs are finite; a program needn't handle non-finite values.
Results may differ from a plain program's by a relative error of at most 0.0054.
Values may be sent and summed in bfloat16 or wider, within the bound.
A program may use at most 128 MiB of HBM per device.

v0:
```python
import functools

import jax
import jax.numpy as jnp
from jax import lax
from jax.experimental import pallas as pl
from jax.experimental.pallas import tpu as pltpu
from jax.sharding import PartitionSpec as P

GROUPS = 32
EPSILON = 1e-05
F32 = jnp.float32
BF16 = jnp.bfloat16
MESH = pl.DeviceIdType.MESH
KERNEL_BYTES = 56 * 1024 * 1024


def bilinear(cols):
    half = cols // 2
    fine = lax.broadcasted_iota(jnp.int32, (cols, cols), 0)
    coarse = lax.broadcasted_iota(jnp.int32, (cols, cols), 1)
    second = coarse >= half
    coarse = jnp.where(second, coarse - half, coarse)
    near = fine // 2
    odd = fine % 2 == 1
    far = jnp.where(odd, jnp.minimum(near + 1, half - 1), jnp.maximum(near - 1, 0))
    value = jnp.where(coarse == near, 0.75, 0.0) + jnp.where(coarse == far, 0.25, 0.0)
    even_rows = value * jnp.where(second, 0.75, 0.25)
    odd_rows = value * jnp.where(second, 0.25, 0.75)
    return even_rows.astype(BF16), odd_rows.astype(BF16)


def mm(a, b):
    return jnp.dot(a, b, preferred_element_type=F32)


def kernel(n, geom, *refs):
    images, chans = geom["images"], geom["chans"]
    rows, cols = geom["rows"], geom["cols"]
    it = iter(refs)
    take = lambda count: [next(it) for _ in range(count)]
    feat_hbm, lat_hbm = take(4), take(4)
    bias, smooth_hbm = take(2)
    conv = take(4)
    sums_two, sums_rest = take(2)
    feat, lat_w = take(4), take(4)
    (smooth,) = take(1)
    big, sends, recvs = take(4), take(4), take(4)
    lats = [None] + take(3)
    ups = take(3)
    stat_two, stat_rest, got_two, got_rest = take(4)
    in_sem, w_sem, s_sem = take(3)
    halo_send, halo_recv, two_send, two_recv, rest_send, rest_recv = take(6)

    me = lax.axis_index("rows")
    first, last = me == 0, me == n - 1

    feat_copy = [pltpu.make_async_copy(feat_hbm[k], feat[k], in_sem.at[k]) for k in range(4)]
    lat_copy = [pltpu.make_async_copy(lat_hbm[k], lat_w[k], w_sem.at[k]) for k in range(4)]
    smooth_copy = [
        pltpu.make_async_copy(smooth_hbm.at[k], smooth.at[k], s_sem.at[k]) for k in range(4)
    ]
    for k in (3, 2, 1, 0):
        lat_copy[k].start()
        feat_copy[k].start()
    for k in (3, 2, 0, 1):
        smooth_copy[k].start()

    barrier = pltpu.get_barrier_semaphore()
    for d in range(1, n):
        pl.semaphore_signal(
            barrier, inc=1, device_id={"rows": lax.rem(me + d, n)}, device_id_type=MESH
        )

    @pl.when(first)
    def _():
        for k in range(4):
            recvs[k][0] = jnp.zeros_like(recvs[k][0])

    @pl.when(last)
    def _():
        for k in range(4):
            recvs[k][1] = jnp.zeros_like(recvs[k][1])

    for k in range(3):
        even, odd = bilinear(cols[k])
        ups[k][0] = even
        ups[k][1] = odd

    def halo_copy(k, way):
        return pltpu.make_async_remote_copy(
            src_ref=sends[k].at[way],
            dst_ref=recvs[k].at[1 - way],
            send_sem=halo_send.at[k, way],
            recv_sem=halo_recv.at[k, 1 - way],
            device_id={"rows": lax.rem(me + (1 if way else n - 1), n)},
            device_id_type=MESH,
        )

    def halo_start(k):
        @pl.when(jnp.logical_not(first))
        def _():
            halo_copy(k, 0).start()

        @pl.when(jnp.logical_not(last))
        def _():
            halo_copy(k, 1).start()

    def halo_wait(k):
        @pl.when(jnp.logical_not(last))
        def _():
            halo_copy(k, 0).wait_recv()

        @pl.when(jnp.logical_not(first))
        def _():
            halo_copy(k, 1).wait_recv()

    def sent_wait(k):
        @pl.when(jnp.logical_not(first))
        def _():
            halo_copy(k, 0).wait_send()

        @pl.when(jnp.logical_not(last))
        def _():
            halo_copy(k, 1).wait_send()

    for k in (3, 2, 1):
        lat_copy[k].wait()
        feat_copy[k].wait()
        for i in range(images):
            flat = feat[k][i].reshape(rows[k] * cols[k], feat[k].shape[-1])
            value = mm(flat, lat_w[k][...]) + bias[k : k + 1, :]
            lats[k][i] = value.reshape(rows[k], cols[k], chans)
            sends[k][0, i] = value[: cols[k]].astype(BF16)
            sends[k][1, i] = value[(rows[k] - 1) * cols[k] :].astype(BF16)
        if k == 3:
            pl.semaphore_wait(barrier, n - 1)
        halo_start(k)
    lat_copy[0].wait()
    feat_copy[0].wait()
    for i in range(images):
        for way, y in ((0, 0), (1, rows[0] - 1)):
            sends[0][way, i] = (mm(feat[0][i, y], lat_w[0][...]) + bias[0:1, :]).astype(BF16)
    halo_start(0)

    def put(k, i, r, value):
        width = cols[k]
        spot = lax.broadcasted_iota(jnp.int32, value.shape, 0)
        before = jnp.where(spot == 0, 0.0, pltpu.roll(value, 1, 0))
        beyond = jnp.where(spot == width - 1, 0.0, pltpu.roll(value, width - 1, 0))
        big[k][i, r, :, 0:chans] = before.astype(BF16)
        big[k][i, r, :, chans : 2 * chans] = value.astype(BF16)
        big[k][i, r, :, 2 * chans :] = beyond.astype(BF16)

    def center(k, i, r):
        return big[k][i, r, :, chans : 2 * chans].astype(F32)

    def doubled(k, i, phase, r):
        pair = big[k + 1][i, pl.ds(r, 2), :, chans : 2 * chans]
        return mm(ups[k][phase], pair.reshape(cols[k], chans))

    for i in range(images):
        for y in range(rows[3]):
            put(3, i, y + 1, lats[3][i, y])
    halo_wait(3)
    for i in range(images):
        put(3, i, 0, jnp.where(first, center(3, i, 1), recvs[3][0, i].astype(F32)))
        put(3, i, rows[3] + 1, jnp.where(last, center(3, i, rows[3]), recvs[3][1, i].astype(F32)))

    def clear(k):
        @pl.when(first)
        def _():
            for i in range(images):
                big[k][i, 0] = jnp.zeros_like(big[k][i, 0])

        @pl.when(last)
        def _():
            for i in range(images):
                big[k][i, rows[k] + 1] = jnp.zeros_like(big[k][i, rows[k] + 1])

    def edges(k):
        for i in range(images):
            above = recvs[k][0, i].astype(F32) + doubled(k, i, 1, 0)
            below = recvs[k][1, i].astype(F32) + doubled(k, i, 0, rows[k] // 2)
            put(k, i, 0, jnp.where(first, center(k, i, 1), above))
            put(k, i, rows[k] + 1, jnp.where(last, center(k, i, rows[k]), below))

    def conv_rows(k, i, y, count):
        total = None
        for a in range(3):
            band = big[k][i, pl.ds(y + a, count)].reshape(count * cols[k], 3 * chans)
            part = mm(band, smooth[k, a])
            total = part if total is None else total + part
        conv[k][i, pl.ds(y, count)] = total.reshape(count, cols[k], chans)
        return jnp.sum(total, 0, keepdims=True), jnp.sum(total * total, 0, keepdims=True)

    stat_rest[...] = jnp.zeros_like(stat_rest)
    stat_two[...] = jnp.zeros_like(stat_two)

    def conv_whole(k):
        smooth_copy[k].wait()
        for i in range(images):
            total, square = conv_rows(k, i, 0, rows[k])
            slot = ((k - 1) * images + i) * 2
            stat_rest[slot : slot + 1, :] = total
            stat_rest[slot + 1 : slot + 2, :] = square

    for k in (2, 1):
        for i in range(images):
            for j in range(rows[k] // 2):
                put(k, i, 2 * j + 1, lats[k][i, 2 * j] + doubled(k, i, 0, j))
                put(k, i, 2 * j + 2, lats[k][i, 2 * j + 1] + doubled(k, i, 1, j + 1))
        if k == 1:
            conv_whole(3)
        halo_wait(k)
        edges(k)
        clear(k + 1)

    pairs = rows[0] // 2

    def merge_two(t, carry):
        i, j = t // pairs, t % pairs
        both = mm(feat[0][i, pl.ds(2 * j, 2)].reshape(2 * cols[0], -1), lat_w[0][...])
        both = both + bias[0:1, :]
        put(0, i, 2 * j + 1, both[: cols[0]] + doubled(0, i, 0, j))
        put(0, i, 2 * j + 2, both[cols[0] :] + doubled(0, i, 1, j + 1))
        return carry

    lax.fori_loop(0, images * pairs, merge_two, 0)

    clear(1)
    conv_whole(2)

    def stat_copies(mine, got, send_sem, recv_sem):
        return [
            pltpu.make_async_remote_copy(
                src_ref=mine,
                dst_ref=got.at[d],
                send_sem=send_sem.at[d],
                recv_sem=recv_sem.at[d],
                device_id={"rows": lax.rem(me + d, n)},
                device_id_type=MESH,
            )
            for d in range(1, n)
        ]

    smooth_copy[0].wait()
    inner = (rows[0] - 2) // 2
    for i in range(images):

        def conv_two(t, carry):
            total, square = conv_rows(0, i, 1 + 2 * t, 2)
            return carry[0] + total, carry[1] + square

        zero = jnp.zeros((1, chans), F32)
        total, square = lax.fori_loop(0, inner, conv_two, (zero, zero))
        stat_two[2 * i : 2 * i + 1, :] = total
        stat_two[2 * i + 1 : 2 * i + 2, :] = square
    conv_whole(1)
    rest_copies = stat_copies(stat_rest, got_rest, rest_send, rest_recv)
    for copy in rest_copies:
        copy.start()
    halo_wait(0)
    edges(0)
    clear(0)

    def conv_edges(t, carry):
        i, y = t // 2, (t % 2) * (rows[0] - 1)
        total, square = conv_rows(0, i, y, 1)
        stat_two[pl.ds(2 * i, 1), :] += total
        stat_two[pl.ds(2 * i + 1, 1), :] += square
        return carry

    lax.fori_loop(0, images * 2, conv_edges, 0)

    two_copies = stat_copies(stat_two, got_two, two_send, two_recv)
    for copy in two_copies:
        copy.start()

    size = chans // GROUPS
    same = lax.broadcasted_iota(jnp.int32, (chans, chans), 0) // size
    same = same == lax.broadcasted_iota(jnp.int32, (chans, chans), 1) // size
    same = jnp.where(same, 1.0, 0.0).astype(F32)

    def gathered(mine, got):
        total = mine[...]
        for d in range(1, n):
            total = total + got[d]
        return jnp.dot(
            total, same, precision=lax.Precision.HIGHEST, preferred_element_type=F32
        )

    for copy in rest_copies:
        copy.wait_recv()
    sums_rest[...] = gathered(stat_rest, got_rest)
    for copy in two_copies:
        copy.wait_recv()
    sums_two[...] = gathered(stat_two, got_two)
    for k in range(4):
        sent_wait(k)
    for copy in two_copies + rest_copies:
        copy.wait_send()


def finish_kernel(n, geom, *refs):
    images, chans = geom["images"], geom["chans"]
    rows, cols = geom["rows"], geom["cols"]
    conv, (sums_two, sums_rest, gain, shift) = refs[0:4], refs[4:8]
    out_hbm, staged, out_sem = refs[8:12], refs[12:16], refs[16]
    size = chans // GROUPS

    def finish(k, i, total, square):
        entries = float(rows[k] * n * cols[k] * size)
        mean = total / entries
        variance = square / entries - mean * mean
        scale = lax.rsqrt(variance + EPSILON) * gain[k : k + 1, :]
        offset = shift[k : k + 1, :]

        def row(y, carry):
            staged[k][i, y] = ((conv[k][i, y] - mean) * scale + offset).astype(BF16)
            return carry

        lax.fori_loop(0, rows[k], row, 0)
        copy = pltpu.make_async_copy(staged[k].at[i], out_hbm[k].at[i], out_sem.at[k, i])
        copy.start()
        return copy

    out_copies = []
    for k in range(4):
        for i in range(images):
            sums = sums_rest if k else sums_two
            slot = (max(k - 1, 0) * images + i) * 2
            out_copies.append(
                finish(k, i, sums[slot : slot + 1, :], sums[slot + 1 : slot + 2, :])
            )
    for copy in out_copies:
        copy.wait()


def per_device(n, *args):
    feats, lat_ws = args[0:4], args[4:8]
    bias, smooth, gain, shift = args[8:12]
    images, chans = feats[0].shape[0], lat_ws[0].shape[1]
    rows = [f.shape[1] for f in feats]
    cols = [f.shape[2] for f in feats]
    geom = {"images": images, "chans": chans, "rows": rows, "cols": cols}
    any_spec = pl.BlockSpec(memory_space=pltpu.HBM)
    vmem_spec = pl.BlockSpec(memory_space=pltpu.VMEM)
    outs = [jax.ShapeDtypeStruct((images, r, c, chans), BF16) for r, c in zip(rows, cols)]
    dma = pltpu.SemaphoreType.DMA
    rest_rows = -(-(3 * images * 2) // 8) * 8
    two_rows = -(-(images * 2) // 8) * 8
    scratch = (
        [pltpu.VMEM(f.shape, BF16) for f in feats]
        + [pltpu.VMEM(w.shape, BF16) for w in lat_ws]
        + [pltpu.VMEM(smooth.shape, BF16)]
        + [pltpu.VMEM((images, r + 2, c, 3 * chans), BF16) for r, c in zip(rows, cols)]
        + [pltpu.VMEM((2, images, c, chans), BF16) for c in cols]
        + [pltpu.VMEM((2, images, c, chans), BF16) for c in cols]
        + [pltpu.VMEM(o.shape, F32) for o in outs[1:]]
        + [pltpu.VMEM((2, c, c), BF16) for c in cols[:3]]
        + [
            pltpu.VMEM((two_rows, chans), F32),
            pltpu.VMEM((rest_rows, chans), F32),
            pltpu.VMEM((n, two_rows, chans), F32),
            pltpu.VMEM((n, rest_rows, chans), F32),
        ]
        + [dma((4,)), dma((4,)), dma((4,))]
        + [dma((4, 2)), dma((4, 2)), dma((n,)), dma((n,)), dma((n,)), dma((n,))]
    )
    held = pl.pallas_call(
        functools.partial(kernel, n, geom),
        out_shape=[pltpu.VMEM(o.shape, F32) for o in outs]
        + [pltpu.VMEM((two_rows, chans), F32), pltpu.VMEM((rest_rows, chans), F32)],
        in_specs=[any_spec] * 8 + [vmem_spec, any_spec],
        out_specs=[vmem_spec] * 6,
        scratch_shapes=scratch,
        compiler_params=pltpu.CompilerParams(
            collective_id=0, has_side_effects=True, vmem_limit_bytes=KERNEL_BYTES
        ),
    )(*args[:10])
    held = [pltpu.with_memory_space_constraint(h, pltpu.VMEM) for h in held]
    return pl.pallas_call(
        functools.partial(finish_kernel, n, geom),
        out_shape=outs,
        in_specs=[vmem_spec] * 8,
        out_specs=[any_spec] * 4,
        scratch_shapes=[pltpu.VMEM(o.shape, BF16) for o in outs] + [dma((4, images))],
        compiler_params=pltpu.CompilerParams(vmem_limit_bytes=16 * 1024 * 1024),
    )(*held, gain, shift)


def solution(mesh):
    strips = P("batch", "rows", None, None)
    run = functools.partial(per_device, mesh.shape["rows"])
    return jax.shard_map(
        lambda *args: tuple(run(*args)),
        mesh=mesh,
        in_specs=(strips,) * 4 + (P(),) * 8,
        out_specs=(strips,) * 4,
        check_vma=False,
    )
```

profile of v0, /device:TPU:0, one launch (start us, length us, event | category | flops | bytes accessed | tf_op | source)
XLA Modules:
  0.0 29.6 jit_solution(8448648271962526424)
XLA Ops:
  0.6 0.0 copy-start.1
  0.6 0.0 copy-start
  0.7 27.1 %shard_map.147 = (f32[2,8,256,256]{3,2,1,0:T(8,128)S(1)}, f32[2,4,128,256]{3,2,1,0:T(8,128)S(1)}, f32[2,2,64,256]{3,2,1,0:T(8,128)S(1)}, f32[2,1,32,256]{3,2,1,0...) custom-call(bf16[2,8,256,256]{3,2,1,0:T(8,128)(2,1)} %refs_0_.1, bf16[2,4,128,512]{3,2,1,0:T(8,128)(2,1)} %refs_1_.1, ...), custom_call_target="tpu_custom_call" | custom-call | tf_op jit(solution)/shard_map/pallas_call | solution.py:371
  27.8 0.0 copy-done.1
  27.8 0.0 copy-done
  27.8 1.9 %shard_map.148 = (bf16[2,8,256,256]{3,2,1,0:T(8,128)(2,1)}, bf16[2,4,128,256]{3,2,1,0:T(8,128)(2,1)}, bf16[2,2,64,256]{3,2,1,0:T(8,128)(2,1)}, bf16[2,1,32,256]{3,2,1,0:T(8,128)(2,1)}) custom-call(f32[2,8,256,256]{3,2,1,0:T(8,128)S(1)} %get-tuple-element.10.refs_0_, f32[2,4,128,256]{3,2,1,0:T(8,128)S(1)} %get-tuple-element.11.refs_1_, ...), custom_call_target="tpu_custom_call" | custom-call | tf_op jit(solution)/shard_map/pallas_call | solution.py:383
Async XLA Ops:
  0.6 27.1 %copy-start.1 = (f32[4,256]{1,0:T(4,128)S(1)}, f32[4,256]{1,0:T(4,128)}, u32[]{:S(2)}) copy-start(f32[4,256]{1,0:T(4,128)} %refs_7_.3) | copy-start | bytes 12292
  0.6 27.1 %copy-start = (f32[4,256]{1,0:T(4,128)S(1)}, f32[4,256]{1,0:T(4,128)}, u32[]{:S(2)}) copy-start(f32[4,256]{1,0:T(4,128)} %refs_6_.3) | copy-start | bytes 12292
where the time goes:
time: 29.8 us; the launch traced here: 29.6 us
  Pallas kernels  29 us (97%)
  between operations  0.68 us (2%)
    pallas_call x1, Pallas kernels, per_device(): pl.pallas_call(functools.partial(kernel, n, geom), out_shape=[pltpu.VMEM(...  27.1 us
    pallas_call x1, Pallas kernels, per_device(): pl.pallas_call(functools.partial(finish_kernel, n, geom), out_shape=outs,...  1.87 us

commit v1 on v0

v1 whole, which is shorter than its diff:
```python
import functools

import jax
import jax.numpy as jnp
from jax import lax
from jax.experimental import pallas as pl
from jax.experimental.pallas import tpu as pltpu
from jax.sharding import PartitionSpec as P

GROUPS = 32
EPSILON = 1e-05
F32 = jnp.float32
BF16 = jnp.bfloat16
MESH = pl.DeviceIdType.MESH
KERNEL_BYTES = 52 * 1024 * 1024
LANES = 128


def bilinear(cols):
    half = cols // 2
    fine = lax.broadcasted_iota(jnp.int32, (cols, cols), 0)
    coarse = lax.broadcasted_iota(jnp.int32, (cols, cols), 1)
    second = coarse >= half
    coarse = jnp.where(second, coarse - half, coarse)
    near = fine // 2
    odd = fine % 2 == 1
    far = jnp.where(odd, jnp.minimum(near + 1, half - 1), jnp.maximum(near - 1, 0))
    value = jnp.where(coarse == near, 0.75, 0.0) + jnp.where(coarse == far, 0.25, 0.0)
    odd_rows = value * jnp.where(second, 0.25, 0.75)
    even_rows = value * jnp.where(second, 0.75, 0.25)
    return odd_rows.astype(BF16), even_rows.astype(BF16)


def mm(a, b):
    return jnp.dot(a, b, preferred_element_type=F32)


def group_totals(value, size):
    parts = []
    for start in range(0, value.shape[1], LANES):
        part = value[:, start : start + LANES]
        lane = lax.broadcasted_iota(jnp.int32, part.shape, 1)
        step = 1
        while step < size:
            upper = (lane // step) % 2 == 1
            other = jnp.where(
                upper, pltpu.roll(part, step, 1), pltpu.roll(part, LANES - step, 1)
            )
            part = part + other
            step *= 2
        parts.append(part)
    return jnp.concatenate(parts, 1)


def kernel(n, geom, *refs):
    images, chans = geom["images"], geom["chans"]
    rows, cols = geom["rows"], geom["cols"]
    it = iter(refs)
    take = lambda count: [next(it) for _ in range(count)]
    feat_hbm, lat_hbm = take(4), take(4)
    bias_hbm, smooth_hbm, gain_hbm, shift_hbm = take(4)
    (conv_two,) = take(1)
    done = [None] + take(3)
    (affine,) = take(1)
    feat, lat_w = take(4), take(4)
    bias, smooth, gain, shift = take(4)
    big, sends, recvs, lats = take(4), [None] + take(3), take(4), take(3)
    conv = [conv_two] + take(3)
    ups, edge, hang = take(3), [None] + take(3), take(1)[0]
    stat_two, stat_rest, got_two, got_rest = take(4)
    in_sem, w_sem, s_sem, p_sem = take(4)
    halo_send, halo_recv, two_send, two_recv, rest_send, rest_recv = take(6)

    me = lax.axis_index("rows")
    first, last = me == 0, me == n - 1
    size = chans // GROUPS

    feat_copy = [pltpu.make_async_copy(feat_hbm[k], feat[k], in_sem.at[k]) for k in range(4)]
    lat_copy = [pltpu.make_async_copy(lat_hbm[k], lat_w[k], w_sem.at[k]) for k in range(4)]
    smooth_copy = [
        pltpu.make_async_copy(smooth_hbm.at[k], smooth.at[k], s_sem.at[k]) for k in range(4)
    ]
    small_copy = [
        pltpu.make_async_copy(src, dst, p_sem.at[j])
        for j, (src, dst) in enumerate(((bias_hbm, bias), (gain_hbm, gain), (shift_hbm, shift)))
    ]
    feat_copy[3].start()
    lat_copy[3].start()
    small_copy[0].start()
    barrier = pltpu.get_barrier_semaphore()
    for d in range(1, n):
        pl.semaphore_signal(
            barrier, inc=1, device_id={"rows": lax.rem(me + d, n)}, device_id_type=MESH
        )
    for k in (2, 1, 0):
        lat_copy[k].start()
        feat_copy[k].start()
    for k in (3, 2, 0, 1):
        smooth_copy[k].start()
    small_copy[1].start()
    small_copy[2].start()

    for k in range(3):
        odd, even = bilinear(cols[k])
        ups[k][0 : cols[k]] = odd
        ups[k][cols[k] :] = even

    def halo_source(k, way):
        if k == 0:
            return feat[0].at[:, way * (rows[0] - 1)]
        return sends[k].at[way * (sends[k].shape[0] - 1)]

    def halo_copy(k, way):
        return pltpu.make_async_remote_copy(
            src_ref=halo_source(k, way),
            dst_ref=recvs[k].at[1 - way],
            send_sem=halo_send.at[k, way],
            recv_sem=halo_recv.at[k, 1 - way],
            device_id={"rows": lax.rem(me + (1 if way else n - 1), n)},
            device_id_type=MESH,
        )

    def halo_start(k):
        @pl.when(jnp.logical_not(first))
        def _():
            halo_copy(k, 0).start()

        @pl.when(jnp.logical_not(last))
        def _():
            halo_copy(k, 1).start()

    def halo_wait(k):
        @pl.when(jnp.logical_not(last))
        def _():
            halo_copy(k, 0).wait_recv()

        @pl.when(jnp.logical_not(first))
        def _():
            halo_copy(k, 1).wait_recv()

    def sent_wait(k):
        @pl.when(jnp.logical_not(first))
        def _():
            halo_copy(k, 0).wait_send()

        @pl.when(jnp.logical_not(last))
        def _():
            halo_copy(k, 1).wait_send()

    small_copy[0].wait()
    feat_copy[3].wait()
    lat_copy[3].wait()
    five = mm(feat[3][...].reshape(-1, feat[3].shape[-1]), lat_w[3][...]) + bias[3:4, :]
    five = five.reshape(images, rows[3], cols[3], chans)
    for y in range(rows[3]):
        sends[3][y] = five[:, y].astype(BF16)
    pl.semaphore_wait(barrier, n - 1)
    halo_start(3)

    lat_copy[2].wait()
    feat_copy[2].wait()
    four = mm(feat[2][...].reshape(-1, feat[2].shape[-1]), lat_w[2][...]) + bias[2:3, :]
    four = four.reshape(images, rows[2], cols[2], chans)
    for y in range(rows[2]):
        lats[2][y] = four[:, y]
    for way, y in ((0, 0), (1, rows[2] - 1)):
        sends[2][way] = four[:, y].astype(BF16)
    halo_start(2)

    lat_copy[1].wait()
    feat_copy[1].wait()
    for y in [0, rows[1] - 1] + list(range(1, rows[1] - 1)):
        for i in range(images):
            value = mm(feat[1][i, y], lat_w[1][...]) + bias[1:2, :]
            lats[1][y, i] = value
            if y in (0, rows[1] - 1):
                sends[1][0 if y == 0 else 1, i] = value.astype(BF16)
        if y == rows[1] - 1:
            halo_start(1)

    lat_copy[0].wait()
    feat_copy[0].wait()
    halo_start(0)
    for y in range(0, rows[0], 2):
        for i in range(images):
            flat = feat[0][i, y : y + 2].reshape(2 * cols[0], -1)
            value = mm(flat, lat_w[0][...]) + bias[0:1, :]
            lats[0][y, i] = value[: cols[0]]
            lats[0][y + 1, i] = value[cols[0] :]

    def put(k, r, i, value):
        width = cols[k]
        spot = lax.broadcasted_iota(jnp.int32, (8, chans), 0)
        before = pltpu.roll(value, 1, 0)
        beyond = pltpu.roll(value, width - 1, 0)
        before = jnp.concatenate([jnp.where(spot == 0, 0.0, before[:8]), before[8:]], 0)
        beyond = jnp.concatenate(
            [beyond[: width - 8], jnp.where(spot == 7, 0.0, beyond[width - 8 :])], 0
        )
        big[k][r, i, :, 0:chans] = before.astype(BF16)
        big[k][r, i, :, chans : 2 * chans] = value.astype(BF16)
        big[k][r, i, :, 2 * chans :] = beyond.astype(BF16)

    def center(k, r, i):
        return big[k][r, i, :, chans : 2 * chans]

    def borders(k, i, above, below):
        if k:
            edge[k][0, i] = jnp.where(first, center(k, 1, i), above.astype(BF16))
            edge[k][1, i] = jnp.where(last, center(k, rows[k], i), below.astype(BF16))
        put(k, 0, i, jnp.where(first, 0.0, above))
        put(k, rows[k] + 1, i, jnp.where(last, 0.0, below))

    def pair(k, p, i):
        upper = edge[k][0, i] if p == 0 else center(k, p, i)
        lower = edge[k][1, i] if p == rows[k] else center(k, p + 1, i)
        return jnp.concatenate([upper, lower], 0)

    def conv_rows(k, y, count):
        bands = [
            big[k][y + a : y + a + count].reshape(count * images * cols[k], 3 * chans)
            for a in range(3)
        ]
        total = mm(jnp.concatenate(bands, 1), smooth[k])
        total = total.reshape(count, images, cols[k], chans)
        sums = []
        for i in range(images):
            part = total[:, i].reshape(-1, 8, chans)
            conv[k][i, y : y + count] = total[:, i]
            sums.append((jnp.sum(part, 0), jnp.sum(part * part, 0)))
        return sums

    def joined(parts):
        total = parts[0]
        for part in parts[1:]:
            total = [(t[0] + u[0], t[1] + u[1]) for t, u in zip(total, part)]
        return total

    def write_sums(dst, start, sums):
        for i in range(images):
            for j in range(2):
                slot = start + 2 * i + j
                dst[slot : slot + 1, :] = jnp.sum(sums[i][j], 0, keepdims=True)

    def spread(mine, got, send_sem, recv_sem):
        return [
            pltpu.make_async_remote_copy(
                src_ref=mine,
                dst_ref=got.at[d],
                send_sem=send_sem.at[d],
                recv_sem=recv_sem.at[d],
                device_id={"rows": lax.rem(me + d, n)},
                device_id_type=MESH,
            )
            for d in range(1, n)
        ]

    stat_rest[...] = jnp.zeros_like(stat_rest)
    stat_two[...] = jnp.zeros_like(stat_two)

    for i in range(images):
        for y in range(rows[3]):
            put(3, y + 1, i, five[i, y])
    halo_wait(3)
    for i in range(images):
        borders(3, i, recvs[3][0, i].astype(F32), recvs[3][1, i].astype(F32))

    outer = {}
    for i in range(images):
        for p in range(rows[3] + 1):
            both = mm(ups[2][...], pair(3, p, i))
            for y, value in ((2 * p - 1, both[: cols[2]]), (2 * p, both[cols[2] :])):
                if 0 <= y < rows[2]:
                    put(2, y + 1, i, lats[2][y, i] + value)
                else:
                    outer[y, i] = value
    smooth_copy[3].wait()
    sums_five = conv_rows(3, 0, rows[3])
    halo_wait(2)
    for i in range(images):
        borders(
            2,
            i,
            recvs[2][0, i].astype(F32) + outer[-1, i],
            recvs[2][1, i].astype(F32) + outer[rows[2], i],
        )

    for p in [*range(1, rows[2]), 0, rows[2]]:
        for i in range(images):
            both = mm(ups[1][...], pair(2, p, i))
            for y, value in ((2 * p - 1, both[: cols[1]]), (2 * p, both[cols[1] :])):
                if 0 <= y < rows[1]:
                    put(1, y + 1, i, lats[1][y, i] + value)
                else:
                    hang[0 if y < 0 else 1, i] = value

    def merge_two(p):
        for i in range(images):
            both = mm(ups[0][...], pair(1, p, i))
            put(0, 2 * p, i, lats[0][2 * p - 1, i] + both[: cols[0]])
            put(0, 2 * p + 1, i, lats[0][2 * p, i] + both[cols[0] :])

    middle = list(range(1, rows[1]))
    merge_two(middle[0])
    smooth_copy[2].wait()
    sums_four = conv_rows(2, 0, rows[2])
    for p in middle[1:2]:
        merge_two(p)
    smooth_copy[0].wait()
    smooth_copy[1].wait()
    sums_two, sums_three = [], []
    sums_three.append(conv_rows(1, 1, rows[1] - 2))
    merged = 2
    for y in range(2, rows[0] - 2):
        while merged < len(middle) and middle[merged - 1] < (y + 2) // 2:
            merge_two(middle[merged])
            merged += 1
        sums_two.append(conv_rows(0, y, 1))

    halo_wait(1)
    for i in range(images):
        borders(
            1,
            i,
            recvs[1][0, i].astype(F32) + hang[0, i],
            recvs[1][1, i].astype(F32) + hang[1, i],
        )
    for i in range(images):
        put(0, 1, i, lats[0][0, i] + mm(ups[0][cols[0] :], pair(1, 0, i)))
        put(0, rows[0], i, lats[0][rows[0] - 1, i] + mm(ups[0][: cols[0]], pair(1, rows[1], i)))
    for y in (0, rows[1] - 1):
        sums_three.append(conv_rows(1, y, 1))
    for start, sums in ((0, sums_three), (1, [sums_four]), (2, [sums_five])):
        write_sums(stat_rest, start * images * 2, joined(sums))
    rest_copies = spread(stat_rest, got_rest, rest_send, rest_recv)
    for copy in rest_copies:
        copy.start()
    for y in (1, rows[0] - 2):
        sums_two.append(conv_rows(0, y, 1))

    halo_wait(0)
    for i in range(images):
        above = mm(
            jnp.concatenate([recvs[0][0, i], ups[0][: cols[0]]], 1),
            jnp.concatenate([lat_w[0][...], pair(1, 0, i)], 0),
        )
        below = mm(
            jnp.concatenate([recvs[0][1, i], ups[0][cols[0] :]], 1),
            jnp.concatenate([lat_w[0][...], pair(1, rows[1], i)], 0),
        )
        borders(0, i, above + bias[0:1, :], below + bias[0:1, :])
    for y in (0, rows[0] - 1):
        sums_two.append(conv_rows(0, y, 1))
    write_sums(stat_two, 0, joined(sums_two))
    two_copies = spread(stat_two, got_two, two_send, two_recv)
    for copy in two_copies:
        copy.start()

    def gathered(mine, got):
        total = mine[...]
        for d in range(1, n):
            total = total + got[d]
        return group_totals(total, size)

    def scales(k, total, square):
        entries = float(rows[k] * n * cols[k] * size)
        mean = total / entries
        variance = square / entries - mean * mean
        scale = lax.rsqrt(variance + EPSILON) * gain[k : k + 1, :]
        return scale, shift[k : k + 1, :] - mean * scale

    small_copy[1].wait()
    small_copy[2].wait()
    for copy in rest_copies:
        copy.wait_recv()
    rest = gathered(stat_rest, got_rest)
    for k in (1, 2, 3):
        for i in range(images):
            slot = ((k - 1) * images + i) * 2
            scale, offset = scales(k, rest[slot : slot + 1], rest[slot + 1 : slot + 2])
            done[k][i] = (conv[k][i] * scale + offset).astype(BF16)

    for copy in two_copies:
        copy.wait_recv()
    two = gathered(stat_two, got_two)
    for i in range(images):
        scale, offset = scales(0, two[2 * i : 2 * i + 1], two[2 * i + 1 : 2 * i + 2])
        affine[2 * i : 2 * i + 1, :] = scale
        affine[2 * i + 1 : 2 * i + 2, :] = offset
    for k in range(4):
        sent_wait(k)
    for copy in two_copies + rest_copies:
        copy.wait_send()


def finish_kernel(geom, *refs):
    images, rows = geom["images"], geom["rows"]
    conv_two, affine = refs[0:2]
    done = [None, *refs[2:5]]
    out_hbm, staged, rest_sem, two_sem = refs[5:9], refs[9], refs[10], refs[11]
    copies = []
    for k in (1, 2, 3):
        copies.append(pltpu.make_async_copy(done[k], out_hbm[k], rest_sem.at[k]))
        copies[-1].start()
    for i in range(images):
        scale = affine[2 * i : 2 * i + 1, :]
        offset = affine[2 * i + 1 : 2 * i + 2, :]
        for y in range(rows[0]):
            staged[i, y] = (conv_two[i, y] * scale + offset).astype(BF16)
            copies.append(
                pltpu.make_async_copy(staged.at[i, y], out_hbm[0].at[i, y], two_sem.at[i, y])
            )
            copies[-1].start()
    for copy in copies:
        copy.wait()


def per_device(n, *args):
    feats, lat_ws = args[0:4], args[4:8]
    bias, smooth, gain, shift = args[8:12]
    smooth = smooth.reshape(smooth.shape[0], -1, smooth.shape[3])
    images, chans = feats[0].shape[0], lat_ws[0].shape[1]
    rows = [f.shape[1] for f in feats]
    cols = [f.shape[2] for f in feats]
    geom = {"images": images, "chans": chans, "rows": rows, "cols": cols}
    any_spec = pl.BlockSpec(memory_space=pltpu.HBM)
    vmem_spec = pl.BlockSpec(memory_space=pltpu.VMEM)
    outs = [jax.ShapeDtypeStruct((images, r, c, chans), BF16) for r, c in zip(rows, cols)]
    dma = pltpu.SemaphoreType.DMA
    rest_rows = -(-(3 * images * 2) // 8) * 8
    two_rows = -(-(images * 2) // 8) * 8
    strip = lambda k, count, width, kind: pltpu.VMEM((count, images, cols[k], width), kind)
    scratch = (
        [pltpu.VMEM(f.shape, BF16) for f in feats]
        + [pltpu.VMEM(w.shape, BF16) for w in lat_ws]
        + [pltpu.VMEM(bias.shape, F32), pltpu.VMEM(smooth.shape, BF16)]
        + [pltpu.VMEM(gain.shape, F32), pltpu.VMEM(shift.shape, F32)]
        + [strip(k, rows[k] + 2, 3 * chans, BF16) for k in range(4)]
        + [strip(k, min(rows[k], 2), chans, BF16) for k in range(1, 4)]
        + [strip(k, 2, chans, BF16) for k in range(4)]
        + [strip(k, rows[k], chans, F32) for k in range(3)]
        + [pltpu.VMEM(o.shape, F32) for o in outs[1:]]
        + [pltpu.VMEM((2 * c, c), BF16) for c in cols[:3]]
        + [strip(k, 2, chans, BF16) for k in range(1, 4)]
        + [strip(1, 2, chans, F32)]
        + [
            pltpu.VMEM((two_rows, chans), F32),
            pltpu.VMEM((rest_rows, chans), F32),
            pltpu.VMEM((n, two_rows, chans), F32),
            pltpu.VMEM((n, rest_rows, chans), F32),
        ]
        + [dma((4,)), dma((4,)), dma((4,)), dma((3,))]
        + [dma((4, 2)), dma((4, 2)), dma((n,)), dma((n,)), dma((n,)), dma((n,))]
    )
    held = pl.pallas_call(
        functools.partial(kernel, n, geom),
        out_shape=[pltpu.VMEM(outs[0].shape, F32)]
        + [pltpu.VMEM(o.shape, BF16) for o in outs[1:]]
        + [pltpu.VMEM((two_rows, chans), F32)],
        in_specs=[any_spec] * 12,
        out_specs=[vmem_spec] * 5,
        scratch_shapes=scratch,
        compiler_params=pltpu.CompilerParams(
            collective_id=0, has_side_effects=True, vmem_limit_bytes=KERNEL_BYTES
        ),
    )(*args[:9], smooth, gain, shift)
    held = [pltpu.with_memory_space_constraint(h, pltpu.VMEM) for h in held]
    return pl.pallas_call(
        functools.partial(finish_kernel, geom),
        out_shape=outs,
        in_specs=[vmem_spec] * 5,
        out_specs=[any_spec] * 4,
        scratch_shapes=[pltpu.VMEM(outs[0].shape, BF16), dma((4,)), dma((images, rows[0]))],
        compiler_params=pltpu.CompilerParams(vmem_limit_bytes=16 * 1024 * 1024),
    )(held[0], held[4], *held[1:4])


def solution(mesh):
    strips = P("batch", "rows", None, None)
    run = functools.partial(per_device, mesh.shape["rows"])
    return jax.shard_map(
        lambda *args: tuple(run(*args)),
        mesh=mesh,
        in_specs=(strips,) * 4 + (P(),) * 8,
        out_specs=(strips,) * 4,
        check_vma=False,
    )
```

time: 29.8 us -> 25 us (0.84)
  Pallas kernels: 29 us -> 24.2 us
    pallas_call x1, Pallas kernels: 27.1 us -> 22.4 us  [per_device(): pl.pallas_call(functools.partial(kernel, n, geom), out_shape=[pltpu.VMEM(...]
where the time goes in v1:
time: 25 us; the launch traced here: 24.8 us
  Pallas kernels  24.2 us (97%)
  between operations  0.64 us (3%)
    pallas_call x1, Pallas kernels, per_device(): pl.pallas_call(functools.partial(kernel, n, geom), out_shape=[pltpu.VMEM(...  22.4 us
    pallas_call x1, Pallas kernels, per_device(): pl.pallas_call(functools.partial(finish_kernel, geom), out_shape=outs, in...  1.73 us

profile of v1, /device:TPU:0, one launch (start us, length us, event | category | flops | bytes accessed | tf_op | source)
XLA Modules:
  0.0 24.8 jit_solution(3833942584898301682)
XLA Ops:
  0.6 22.4 %shard_map.147 = (f32[2,8,256,256]{3,2,1,0:T(8,128)S(1)}, bf16[2,4,128,256]{3,2,1,0:T(8,128)(2,1)S(1)}, bf16[2,2,64,256]{3,2,1,0:T(8,128)(2,1)S(1)}, bf16[2,1,32,256]{3,2,1,0:T(8,128)(2,1)S(1)}, f32[8,256]{1,0:T(8,128)S(1)}) custom-call(bf16[2,8,256,256]{3,2,1,0:T(8,128)(2,1)} %refs_0_.1, bf16[2,4,128,512]{3,2,1,0:T(8,128)(2,1)} %refs_1_.1, ...), custom_call_target="tpu_custom_call" | custom-call | tf_op jit(solution)/shard_map/pallas_call | solution.py:455
  23.1 1.7 %shard_map.148 = (bf16[2,8,256,256]{3,2,1,0:T(8,128)(2,1)}, bf16[2,4,128,256]{3,2,1,0:T(8,128)(2,1)}, bf16[2,2,64,256]{3,2,1,0:T(8,128)(2,1)}, bf16[2,1,32,256]{3,2,1,0:T(8,128)(2,1)}) custom-call(f32[2,8,256,256]{3,2,1,0:T(8,128)S(1)} %get-tuple-element.9.refs_0_, f32[8,256]{1,0:T(8,128)S(1)} %get-tuple-element.10.refs_1_, ...), custom_call_target="tpu_custom_call" | custom-call | tf_op jit(solution)/shard_map/pallas_call | solution.py:468

commit v2 on v1

--- a/solution.py
+++ b/solution.py
@@ -33,6 +33,11 @@
 
 def mm(a, b):
     return jnp.dot(a, b, preferred_element_type=F32)
+
+
+def mm_halves(a, b, step):
+    cut = -(-(a.shape[1] // step) // 2) * step
+    return mm(a[:, :cut], b[:cut]) + mm(a[:, cut:], b[cut:])
 
 
 def group_totals(value, size):
@@ -77,9 +82,7 @@
 
     feat_copy = [pltpu.make_async_copy(feat_hbm[k], feat[k], in_sem.at[k]) for k in range(4)]
     lat_copy = [pltpu.make_async_copy(lat_hbm[k], lat_w[k], w_sem.at[k]) for k in range(4)]
-    smooth_copy = [
-        pltpu.make_async_copy(smooth_hbm.at[k], smooth.at[k], s_sem.at[k]) for k in range(4)
-    ]
+    smooth_copy = pltpu.make_async_copy(smooth_hbm, smooth, s_sem.at[0])
     small_copy = [
         pltpu.make_async_copy(src, dst, p_sem.at[j])
         for j, (src, dst) in enumerate(((bias_hbm, bias), (gain_hbm, gain), (shift_hbm, shift)))
@@ -95,8 +98,7 @@
     for k in (2, 1, 0):
         lat_copy[k].start()
         feat_copy[k].start()
-    for k in (3, 2, 0, 1):
-        smooth_copy[k].start()
+    smooth_copy.start()
     small_copy[1].start()
     small_copy[2].start()
 
@@ -150,7 +152,8 @@
     small_copy[0].wait()
     feat_copy[3].wait()
     lat_copy[3].wait()
-    five = mm(feat[3][...].reshape(-1, feat[3].shape[-1]), lat_w[3][...]) + bias[3:4, :]
+    flat = feat[3][...].reshape(-1, feat[3].shape[-1])
+    five = mm_halves(flat, lat_w[3], chans) + bias[3:4, :]
     five = five.reshape(images, rows[3], cols[3], chans)
     for y in range(rows[3]):
         sends[3][y] = five[:, y].astype(BF16)
@@ -159,24 +162,29 @@
 
     lat_copy[2].wait()
     feat_copy[2].wait()
-    four = mm(feat[2][...].reshape(-1, feat[2].shape[-1]), lat_w[2][...]) + bias[2:3, :]
-    four = four.reshape(images, rows[2], cols[2], chans)
-    for y in range(rows[2]):
-        lats[2][y] = four[:, y]
-    for way, y in ((0, 0), (1, rows[2] - 1)):
-        sends[2][way] = four[:, y].astype(BF16)
+    for i in range(images):
+        flat = feat[2][i].reshape(rows[2] * cols[2], -1)
+        value = (mm(flat, lat_w[2][...]) + bias[2:3, :]).reshape(rows[2], cols[2], chans)
+        for y in range(rows[2]):
+            lats[2][y, i] = value[y]
+        sends[2][0, i] = value[0].astype(BF16)
+        sends[2][1, i] = value[rows[2] - 1].astype(BF16)
     halo_start(2)
 
     lat_copy[1].wait()
     feat_copy[1].wait()
-    for y in [0, rows[1] - 1] + list(range(1, rows[1] - 1)):
-        for i in range(images):
-            value = mm(feat[1][i, y], lat_w[1][...]) + bias[1:2, :]
-            lats[1][y, i] = value
-            if y in (0, rows[1] - 1):
-                sends[1][0 if y == 0 else 1, i] = value.astype(BF16)
-        if y == rows[1] - 1:
-            halo_start(1)
+    def lateral_three(some):
+        for i in range(images):
+            flat = jnp.concatenate([feat[1][i, y] for y in some], 0)
+            value = (mm(flat, lat_w[1][...]) + bias[1:2, :]).reshape(len(some), cols[1], chans)
+            for j, y in enumerate(some):
+                lats[1][y, i] = value[j]
+                if y in (0, rows[1] - 1):
+                    sends[1][0 if y == 0 else 1, i] = value[j].astype(BF16)
+
+    lateral_three([0, rows[1] - 1])
+    halo_start(1)
+    lateral_three(list(range(1, rows[1] - 1)))
 
     lat_copy[0].wait()
     feat_copy[0].wait()
@@ -216,17 +224,30 @@
         lower = edge[k][1, i] if p == rows[k] else center(k, p + 1, i)
         return jnp.concatenate([upper, lower], 0)
 
-    def conv_rows(k, y, count):
-        bands = [
-            big[k][y + a : y + a + count].reshape(count * images * cols[k], 3 * chans)
-            for a in range(3)
-        ]
-        total = mm(jnp.concatenate(bands, 1), smooth[k])
-        total = total.reshape(count, images, cols[k], chans)
+    def conv_rows(k, some, split=False):
         sums = []
-        for i in range(images):
-            part = total[:, i].reshape(-1, 8, chans)
-            conv[k][i, y : y + count] = total[:, i]
+        if split:
+            stacked = [
+                jnp.concatenate(
+                    [big[k][y + a, i] for y in some for i in range(images)], 0
+                )
+                for a in range(3)
+            ]
+            total = mm_halves(jnp.concatenate(stacked, 1), smooth.at[k], chans)
+            total = total.reshape(len(some), images, cols[k], chans)
+            values = [total[:, i] for i in range(images)]
+        else:
+            values = []
+            for i in range(images):
+                stacked = [
+                    jnp.concatenate([big[k][y + a, i] for y in some], 0) for a in range(3)
+                ]
+                total = mm(jnp.concatenate(stacked, 1), smooth[k])
+                values.append(total.reshape(len(some), cols[k], chans))
+        for i in range(images):
+            for j, y in enumerate(some):
+                conv[k][i, y] = values[i][j]
+            part = values[i].reshape(-1, 8, chans)
             sums.append((jnp.sum(part, 0), jnp.sum(part * part, 0)))
         return sums
 
@@ -246,17 +267,22 @@
         return [
             pltpu.make_async_remote_copy(
                 src_ref=mine,
-                dst_ref=got.at[d],
-                send_sem=send_sem.at[d],
-                recv_sem=recv_sem.at[d],
+                dst_ref=got.at[d - 1],
+                send_sem=send_sem.at[0],
+                recv_sem=recv_sem.at[0],
                 device_id={"rows": lax.rem(me + d, n)},
                 device_id_type=MESH,
             )
             for d in range(1, n)
         ]
 
+    def all_of(got, sem):
+        pltpu.make_async_copy(got, got, sem.at[0]).wait()
+
     stat_rest[...] = jnp.zeros_like(stat_rest)
     stat_two[...] = jnp.zeros_like(stat_two)
+
+    smooth_copy.wait()
 
     for i in range(images):
         for y in range(rows[3]):
@@ -266,16 +292,14 @@
         borders(3, i, recvs[3][0, i].astype(F32), recvs[3][1, i].astype(F32))
 
     outer = {}
-    for i in range(images):
-        for p in range(rows[3] + 1):
+    for p in range(rows[3] + 1):
+        for i in range(images):
             both = mm(ups[2][...], pair(3, p, i))
             for y, value in ((2 * p - 1, both[: cols[2]]), (2 * p, both[cols[2] :])):
                 if 0 <= y < rows[2]:
                     put(2, y + 1, i, lats[2][y, i] + value)
                 else:
                     outer[y, i] = value
-    smooth_copy[3].wait()
-    sums_five = conv_rows(3, 0, rows[3])
     halo_wait(2)
     for i in range(images):
         borders(
@@ -285,7 +309,7 @@
             recvs[2][1, i].astype(F32) + outer[rows[2], i],
         )
 
-    for p in [*range(1, rows[2]), 0, rows[2]]:
+    def merge_three(p):
         for i in range(images):
             both = mm(ups[1][...], pair(2, p, i))
             for y, value in ((2 * p - 1, both[: cols[1]]), (2 * p, both[cols[1] :])):
@@ -300,22 +324,26 @@
             put(0, 2 * p, i, lats[0][2 * p - 1, i] + both[: cols[0]])
             put(0, 2 * p + 1, i, lats[0][2 * p, i] + both[cols[0] :])
 
-    middle = list(range(1, rows[1]))
-    merge_two(middle[0])
-    smooth_copy[2].wait()
-    sums_four = conv_rows(2, 0, rows[2])
-    for p in middle[1:2]:
-        merge_two(p)
-    smooth_copy[0].wait()
-    smooth_copy[1].wait()
-    sums_two, sums_three = [], []
-    sums_three.append(conv_rows(1, 1, rows[1] - 2))
-    merged = 2
-    for y in range(2, rows[0] - 2):
-        while merged < len(middle) and middle[merged - 1] < (y + 2) // 2:
-            merge_two(middle[merged])
+    for p in range(1, rows[2]):
+        merge_three(p)
+    sums_five = conv_rows(3, list(range(rows[3])), True)
+    merge_three(0)
+    merge_three(rows[2])
+    merge_two(1)
+    sums_four = conv_rows(2, list(range(rows[2])))
+    sums_three = [conv_rows(1, list(range(1, rows[1] - 1)))]
+    merged, sums_two = 1, []
+
+    def conv_two_row(y):
+        nonlocal merged
+        while merged < min((y + 2) // 2, rows[1] - 1):
             merged += 1
-        sums_two.append(conv_rows(0, y, 1))
+            merge_two(merged)
+        sums_two.append(conv_rows(0, [y]))
+
+    inner = list(range(2, rows[0] - 2))
+    for y in inner[: len(inner) // 2]:
+        conv_two_row(y)
 
     halo_wait(1)
     for i in range(images):
@@ -327,30 +355,34 @@
         )
     for i in range(images):
         put(0, 1, i, lats[0][0, i] + mm(ups[0][cols[0] :], pair(1, 0, i)))
+    for i in range(images):
         put(0, rows[0], i, lats[0][rows[0] - 1, i] + mm(ups[0][: cols[0]], pair(1, rows[1], i)))
-    for y in (0, rows[1] - 1):
-        sums_three.append(conv_rows(1, y, 1))
+    for y in inner[len(inner) // 2 :]:
+        conv_two_row(y)
+    sums_three.append(conv_rows(1, [0, rows[1] - 1]))
     for start, sums in ((0, sums_three), (1, [sums_four]), (2, [sums_five])):
         write_sums(stat_rest, start * images * 2, joined(sums))
+    conv_two_row(1)
+    conv_two_row(rows[0] - 2)
+
     rest_copies = spread(stat_rest, got_rest, rest_send, rest_recv)
     for copy in rest_copies:
         copy.start()
-    for y in (1, rows[0] - 2):
-        sums_two.append(conv_rows(0, y, 1))
-
     halo_wait(0)
-    for i in range(images):
-        above = mm(
-            jnp.concatenate([recvs[0][0, i], ups[0][: cols[0]]], 1),
-            jnp.concatenate([lat_w[0][...], pair(1, 0, i)], 0),
-        )
-        below = mm(
-            jnp.concatenate([recvs[0][1, i], ups[0][cols[0] :]], 1),
-            jnp.concatenate([lat_w[0][...], pair(1, rows[1], i)], 0),
-        )
-        borders(0, i, above + bias[0:1, :], below + bias[0:1, :])
-    for y in (0, rows[0] - 1):
-        sums_two.append(conv_rows(0, y, 1))
+    sides = []
+    for way, half, p in ((0, ups[0][: cols[0]], 0), (1, ups[0][cols[0] :], rows[1])):
+        for i in range(images):
+            sides.append(
+                mm(
+                    jnp.concatenate([recvs[0][way, i], half], 1),
+                    jnp.concatenate([lat_w[0][...], pair(1, p, i)], 0),
+                )
+                + bias[0:1, :]
+            )
+    for i in range(images):
+        borders(0, i, sides[i], sides[images + i])
+    conv_two_row(0)
+    conv_two_row(rows[0] - 1)
     write_sums(stat_two, 0, joined(sums_two))
     two_copies = spread(stat_two, got_two, two_send, two_recv)
     for copy in two_copies:
@@ -358,21 +390,20 @@
 
     def gathered(mine, got):
         total = mine[...]
-        for d in range(1, n):
+        for d in range(n - 1):
             total = total + got[d]
         return group_totals(total, size)
 
     def scales(k, total, square):
-        entries = float(rows[k] * n * cols[k] * size)
-        mean = total / entries
-        variance = square / entries - mean * mean
+        share = 1.0 / float(rows[k] * n * cols[k] * size)
+        mean = total * share
+        variance = square * share - mean * mean
         scale = lax.rsqrt(variance + EPSILON) * gain[k : k + 1, :]
         return scale, shift[k : k + 1, :] - mean * scale
 
     small_copy[1].wait()
     small_copy[2].wait()
-    for copy in rest_copies:
-        copy.wait_recv()
+    all_of(got_rest, rest_recv)
     rest = gathered(stat_rest, got_rest)
     for k in (1, 2, 3):
         for i in range(images):
@@ -380,8 +411,7 @@
             scale, offset = scales(k, rest[slot : slot + 1], rest[slot + 1 : slot + 2])
             done[k][i] = (conv[k][i] * scale + offset).astype(BF16)
 
-    for copy in two_copies:
-        copy.wait_recv()
+    all_of(got_two, two_recv)
     two = gathered(stat_two, got_two)
     for i in range(images):
         scale, offset = scales(0, two[2 * i : 2 * i + 1], two[2 * i + 1 : 2 * i + 2])
@@ -389,8 +419,8 @@
         affine[2 * i + 1 : 2 * i + 2, :] = offset
     for k in range(4):
         sent_wait(k)
-    for copy in two_copies + rest_copies:
-        copy.wait_send()
+    all_of(got_rest, rest_send)
+    all_of(got_two, two_send)
 
 
 def finish_kernel(geom, *refs):
@@ -407,12 +437,12 @@
         offset = affine[2 * i + 1 : 2 * i + 2, :]
         for y in range(rows[0]):
             staged[i, y] = (conv_two[i, y] * scale + offset).astype(BF16)
-            copies.append(
-                pltpu.make_async_copy(staged.at[i, y], out_hbm[0].at[i, y], two_sem.at[i, y])
-            )
-            copies[-1].start()
+            pltpu.make_async_copy(
+                staged.at[i, y], out_hbm[0].at[i, y], two_sem.at[0]
+            ).start()
     for copy in copies:
         copy.wait()
+    pltpu.make_async_copy(staged, out_hbm[0], two_sem.at[0]).wait()
 
 
 def per_device(n, *args):
@@ -446,11 +476,11 @@
         + [
             pltpu.VMEM((two_rows, chans), F32),
             pltpu.VMEM((rest_rows, chans), F32),
-            pltpu.VMEM((n, two_rows, chans), F32),
-            pltpu.VMEM((n, rest_rows, chans), F32),
+            pltpu.VMEM((n - 1, two_rows, chans), F32),
+            pltpu.VMEM((n - 1, rest_rows, chans), F32),
         ]
-        + [dma((4,)), dma((4,)), dma((4,)), dma((3,))]
-        + [dma((4, 2)), dma((4, 2)), dma((n,)), dma((n,)), dma((n,)), dma((n,))]
+        + [dma((4,)), dma((4,)), dma((1,)), dma((3,))]
+        + [dma((4, 2)), dma((4, 2)), dma((1,)), dma((1,)), dma((1,)), dma((1,))]
     )
     held = pl.pallas_call(
         functools.partial(kernel, n, geom),
@@ -470,7 +500,7 @@
         out_shape=outs,
         in_specs=[vmem_spec] * 5,
         out_specs=[any_spec] * 4,
-        scratch_shapes=[pltpu.VMEM(outs[0].shape, BF16), dma((4,)), dma((images, rows[0]))],
+        scratch_shapes=[pltpu.VMEM(outs[0].shape, BF16), dma((4,)), dma((1,))],
         compiler_params=pltpu.CompilerParams(vmem_limit_bytes=16 * 1024 * 1024),
     )(held[0], held[4], *held[1:4])
 

time: 25 us -> 23.4 us (0.936)
  Pallas kernels: 24.2 us -> 22.6 us
    pallas_call x1, Pallas kernels: 22.4 us -> 21 us  [per_device(): pl.pallas_call(functools.partial(kernel, n, geom), out_shape=[pltpu.VMEM(...]
where the time goes in v2:
time: 23.4 us; the launch traced here: 23.2 us
  Pallas kernels  22.6 us (97%)
  between operations  0.64 us (3%)
    pallas_call x1, Pallas kernels, per_device(): pl.pallas_call(functools.partial(kernel, n, geom), out_shape=[pltpu.VMEM(...  21 us
    pallas_call x1, Pallas kernels, per_device(): pl.pallas_call(functools.partial(finish_kernel, geom), out_shape=outs, in...  1.59 us

profile of v2, /device:TPU:0, one launch (start us, length us, event | category | flops | bytes accessed | tf_op | source)
XLA Modules:
  0.0 23.2 jit_solution(12951590422991328408)
XLA Ops:
  0.6 21.0 %shard_map.147 = (f32[2,8,256,256]{3,2,1,0:T(8,128)S(1)}, bf16[2,4,128,256]{3,2,1,0:T(8,128)(2,1)S(1)}, bf16[2,2,64,256]{3,2,1,0:T(8,128)(2,1)S(1)}, bf16[2,1,32,256]{3,2,1,0:T(8,128)(2,1)S(1)}, f32[8,256]{1,0:T(8,128)S(1)}) custom-call(bf16[2,8,256,256]{3,2,1,0:T(8,128)(2,1)} %refs_0_.1, bf16[2,4,128,512]{3,2,1,0:T(8,128)(2,1)} %refs_1_.1, ...), custom_call_target="tpu_custom_call" | custom-call | tf_op jit(solution)/shard_map/pallas_call | solution.py:485
  21.6 1.6 %shard_map.148 = (bf16[2,8,256,256]{3,2,1,0:T(8,128)(2,1)}, bf16[2,4,128,256]{3,2,1,0:T(8,128)(2,1)}, bf16[2,2,64,256]{3,2,1,0:T(8,128)(2,1)}, bf16[2,1,32,256]{3,2,1,0:T(8,128)(2,1)}) custom-call(f32[2,8,256,256]{3,2,1,0:T(8,128)S(1)} %get-tuple-element.9.refs_0_, f32[8,256]{1,0:T(8,128)S(1)} %get-tuple-element.10.refs_1_, ...), custom_call_target="tpu_custom_call" | custom-call | tf_op jit(solution)/shard_map/pallas_call | solution.py:498

commit v3 on v2

v3 whole, which is shorter than its diff:
```python
import functools
import math

import jax
import jax.numpy as jnp
from jax import lax
from jax.experimental import pallas as pl
from jax.experimental.pallas import tpu as pltpu
from jax.sharding import PartitionSpec as P

GROUPS = 32
EPSILON = 1e-05
F32 = jnp.float32
BF16 = jnp.bfloat16
MESH = pl.DeviceIdType.MESH
KERNEL_BYTES = 52 * 1024 * 1024
LANES = 128


def halves_first(index, width, split):
    if not split:
        return index
    return 2 * (index % (width // 2)) + index // (width // 2)


def bilinear(cols, fine_split, coarse_split):
    half = cols // 2
    fine = halves_first(lax.broadcasted_iota(jnp.int32, (cols, cols), 0), cols, fine_split)
    place = lax.broadcasted_iota(jnp.int32, (cols, cols), 1)
    second = place >= half
    coarse = halves_first(jnp.where(second, place - half, place), half, coarse_split)
    near = fine // 2
    odd = fine % 2 == 1
    far = jnp.where(odd, jnp.minimum(near + 1, half - 1), jnp.maximum(near - 1, 0))
    value = jnp.where(coarse == near, 0.75, 0.0) + jnp.where(coarse == far, 0.25, 0.0)
    odd_rows = value * jnp.where(second, 0.25, 0.75)
    even_rows = value * jnp.where(second, 0.75, 0.25)
    return odd_rows.astype(BF16), even_rows.astype(BF16)


def mm(a, b):
    return jnp.dot(a, b, preferred_element_type=F32)


def mm_halves(start, a, b, step):
    cut = -(-(a.shape[1] // step) // 2) * step
    return (start + mm(a[:, :cut], b[:cut])) + mm(a[:, cut:], b[cut:])


def group_totals(value, size):
    parts = []
    for start in range(0, value.shape[1], LANES):
        part = value[:, start : start + LANES]
        spot = lax.broadcasted_iota(jnp.int32, part.shape, 1) % size
        terms = [part]
        for step in range(1, size):
            terms.append(
                jnp.where(
                    spot >= step,
                    pltpu.roll(part, step, 1),
                    pltpu.roll(part, LANES + step - size, 1),
                )
            )
        while len(terms) > 1:
            terms = [sum(terms[j : j + 2]) for j in range(0, len(terms), 2)]
        parts.append(terms[0])
    return jnp.concatenate(parts, 1)


def own_slots(shape, size):
    row = lax.broadcasted_iota(jnp.int32, shape, 0)
    return lax.broadcasted_iota(jnp.int32, shape, 1) % size == row


def packed(stats, size):
    value = jnp.concatenate(stats, 0)
    value = jnp.where(own_slots(value.shape, size), group_totals(value, size), 0.0)
    return jnp.sum(value, 0, keepdims=True)


def unpacked(row, size):
    value = jnp.broadcast_to(row, (size, row.shape[1]))
    return group_totals(jnp.where(own_slots(value.shape, size), value, 0.0), size)


def kernel(n, geom, *refs):
    images, chans = geom["images"], geom["chans"]
    rows, cols = geom["rows"], geom["cols"]
    it = iter(refs)
    take = lambda count: [next(it) for _ in range(count)]
    feat_hbm, lat_hbm = take(4), take(4)
    consts_hbm, smooth_hbm = take(3), take(1)[0]
    (conv_two,) = take(1)
    done = [None] + take(3)
    (affine,) = take(1)
    feat, lat_w = take(4), take(4)
    consts, smooth, mixed = take(3)
    vee, big = take(2), [None, None] + take(2)
    sends, recvs, lats = [None] + take(3), take(4), take(3)
    conv = [conv_two] + take(3)
    ups, edge, hang = take(3), [None] + take(3), take(2)
    mid, hop = take(2)
    box_two, box_rest = take(2)
    in_sem, w_sem, s_sem, p_sem = take(4)
    halo_send, halo_recv, hop_send, hop_recv = take(4)
    two_send, two_recv, rest_send, rest_recv = take(4)
    bias, gain, shift = (consts.at[j] for j in range(3))

    me = lax.axis_index("rows")
    first, last = me == 0, me == n - 1
    size, blocks = chans // GROUPS, chans // LANES
    half = [c // 2 for c in cols]
    top = [r + 1 for r in rows]

    feat_copy = [pltpu.make_async_copy(feat_hbm[k], feat[k], in_sem.at[k]) for k in range(4)]
    lat_copy = [pltpu.make_async_copy(lat_hbm[k], lat_w[k], w_sem.at[k]) for k in range(4)]
    smooth_copy = [
        pltpu.make_async_copy(
            smooth_hbm.at[2 * j : 2 * j + 2], smooth.at[2 * j : 2 * j + 2], s_sem.at[j]
        )
        for j in range(2)
    ]
    feat_copy[3].start()
    lat_copy[3].start()
    for j in range(3):
        pltpu.make_async_copy(consts_hbm[j], consts.at[j], p_sem.at[0]).start()
    barrier = pltpu.get_barrier_semaphore()
    for d in range(1, n):
        pl.semaphore_signal(
            barrier, inc=1, device_id={"rows": lax.rem(me + d, n)}, device_id_type=MESH
        )
    for k in (2, 1, 0):
        lat_copy[k].start()
        feat_copy[k].start()
    for copy in smooth_copy:
        copy.start()

    for k in range(3):
        odd, even = bilinear(cols[k], k < 2, k == 0)
        ups[k][0 : cols[k]] = odd
        ups[k][cols[k] :] = even

    def remote(src, dst, send_sem, recv_sem, shift_by):
        return pltpu.make_async_remote_copy(
            src_ref=src,
            dst_ref=dst,
            send_sem=send_sem,
            recv_sem=recv_sem,
            device_id={"rows": lax.rem(me + (n + shift_by), n)},
            device_id_type=MESH,
        )

    def halo_source(k, way):
        if k == 0:
            return feat[0].at[:, way * (rows[0] - 1)]
        return sends[k].at[way * (sends[k].shape[0] - 1)]

    def halo_copy(k, way):
        return remote(
            halo_source(k, way),
            recvs[k].at[1 - way],
            halo_send.at[k, way],
            halo_recv.at[k, 1 - way],
            1 if way else -1,
        )

    def on_ends(act):
        @pl.when(jnp.logical_not(first))
        def _():
            act(0)

        @pl.when(jnp.logical_not(last))
        def _():
            act(1)

    def halo_start(k):
        on_ends(lambda way: halo_copy(k, way).start())

    def halo_wait(k):
        on_ends(lambda way: halo_copy(k, 1 - way).wait_recv())

    span = 2 * max(1, math.isqrt(n // 2))
    early = images // 2
    pieces = ((0, early), (early, images)) if early else ((0, images), (0, images))
    place = lax.rem(me, span)
    crosses = (
        jnp.logical_and(place == 0, jnp.logical_not(first)),
        jnp.logical_and(place == span - 1, jnp.logical_not(last)),
    )
    carries = (
        jnp.logical_and(place == 0, me + span < n),
        jnp.logical_and(place == span - 1, me >= span),
    )
    relays = span < n
    hops = range(2) if early else range(1, 2)

    def fine_start():
        def begin(way):
            if not relays:
                halo_copy(0, way).start()
                return

            @pl.when(jnp.logical_not(crosses[way]))
            def _():
                halo_copy(0, way).start()

            @pl.when(crosses[way])
            def _():
                for j in hops:
                    here = slice(*pieces[j])
                    remote(
                        feat[0].at[here, way * (rows[0] - 1)],
                        hop.at[here],
                        halo_send.at[0, way],
                        hop_recv.at[j],
                        span if way else -span,
                    ).start()

        on_ends(begin)

    def carry(act):
        if relays:
            for way in range(2):
                pl.when(carries[way])(functools.partial(act, way))

    def carry_start(j):
        def act(way):
            here = hop.at[slice(*pieces[j])]
            pltpu.make_async_copy(here, here, hop_recv.at[j]).wait()
            remote(
                here,
                recvs[0].at[1 - way, slice(*pieces[j])],
                hop_send.at[0],
                halo_recv.at[0, 1 - way],
                1 - span if way else span - 1,
            ).start()

        if j in hops:
            carry(act)

    pltpu.make_async_copy(consts, consts, p_sem.at[0]).wait()
    feat_copy[3].wait()
    lat_copy[3].wait()
    flat = feat[3][...].reshape(-1, feat[3].shape[-1])
    five = mm_halves(bias[3:4, :], flat, lat_w[3], chans)
    five = five.reshape(images, rows[3], cols[3], chans)
    for y in range(rows[3]):
        sends[3][y] = five[:, y].astype(BF16)
    pl.semaphore_wait(barrier, n - 1)
    halo_start(3)

    lat_copy[2].wait()
    feat_copy[2].wait()
    for i in range(images):
        flat = feat[2][i].reshape(rows[2] * cols[2], -1)
        value = (bias[2:3, :] + mm(flat, lat_w[2][...])).reshape(rows[2], cols[2], chans)
        for y in range(rows[2]):
            lats[2][y, i] = value[y]
        sends[2][0, i] = value[0].astype(BF16)
        sends[2][1, i] = value[rows[2] - 1].astype(BF16)
    halo_start(2)

    def columns(k, r, i):
        return [
            jnp.concatenate(
                [lats[k][r, i, b, pl.ds(odd, half[k], stride=2), :] for b in range(blocks)], 1
            )
            for odd in range(2)
        ]

    def keep(k, r, i, value):
        for b in range(blocks):
            lats[k][r, i, b] = value[:, b * LANES : (b + 1) * LANES]

    lat_copy[1].wait()
    feat_copy[1].wait()

    def lateral_three(some):
        for i in range(images):
            flat = jnp.concatenate([feat[1][i, y] for y in some], 0)
            value = (bias[1:2, :] + mm(flat, lat_w[1][...])).reshape(len(some), cols[1], chans)
            for j, y in enumerate(some):
                keep(1, y, i, value[j])
        for y in some:
            if y in (0, rows[1] - 1):
                for i in range(images):
                    even, odd = columns(1, y, i)
                    sends[1][0 if y == 0 else 1, i, : half[1]] = even.astype(BF16)
                    sends[1][0 if y == 0 else 1, i, half[1] :] = odd.astype(BF16)

    lateral_three([0, rows[1] - 1])
    halo_start(1)
    lateral_three(list(range(1, rows[1] - 1)))

    def lateral_two(y):
        for i in range(images):
            flat = feat[0][i, y : y + 2].reshape(2 * cols[0], -1)
            value = bias[0:1, :] + mm(flat, lat_w[0][...])
            keep(0, y + 1, i, value[: cols[0]])
            keep(0, y + 2, i, value[cols[0] :])

    lat_copy[0].wait()
    feat_copy[0].wait()
    fine_start()
    steps = list(range(0, rows[0], 2))
    for y in steps[: len(steps) // 2]:
        lateral_two(y)

    def tap(k, a, b, start=0, count=chans):
        return smooth[k, pl.ds((3 * a + b) * chans + start, count)]

    smooth_copy[0].wait()
    piece = 16

    def mix(k, a, start):
        taps = [tap(k, a, b, start, piece).astype(F32) for b in range(3)]
        outer_taps, inner_tap = (taps[0] + taps[2]) * 0.5, taps[1] * 0.5
        mixed[k, 0, pl.ds(a * chans + start, piece)] = (outer_taps + inner_tap).astype(BF16)
        mixed[k, 1, pl.ds(a * chans + start, piece)] = (outer_taps - inner_tap).astype(BF16)

    for k in range(2):
        for a in range(3):
            for start in range(0, chans, piece):
                mix(k, a, start)
    for y in steps[len(steps) // 2 :]:
        lateral_two(y)
    smooth_copy[1].wait()

    def moved(value, by):
        length = value.shape[0]
        spot = lax.broadcasted_iota(jnp.int32, (8, value.shape[1]), 0)
        if by > 0:
            value = pltpu.roll(value, 1, 0)
            return jnp.concatenate([jnp.where(spot == 0, 0.0, value[:8]), value[8:]], 0)
        value = pltpu.roll(value, length - 1, 0)
        cut = length - 8
        return jnp.concatenate([value[:cut], jnp.where(spot == 7, 0.0, value[cut:])], 0)

    def put(k, r, i, value):
        big[k][r, i, :, 0:chans] = moved(value, 1).astype(BF16)
        big[k][r, i, :, chans : 2 * chans] = value.astype(BF16)
        big[k][r, i, :, 2 * chans :] = moved(value, -1).astype(BF16)

    def put_pairs(k, r, i, even, odd):
        vee[k][r, 0, i] = (moved(odd, 1) - odd).astype(BF16)
        vee[k][r, 1, i] = (even + odd).astype(BF16)
        vee[k][r, 2, i] = (odd - even).astype(BF16)
        vee[k][r, 3, i] = (even - moved(even, -1)).astype(BF16)

    def center(k, r, i):
        return big[k][r, i, :, chans : 2 * chans]

    def borders(k, i, above, below):
        edge[k][0, i] = jnp.where(first, center(k, 1, i), above.astype(BF16))
        edge[k][1, i] = jnp.where(last, center(k, rows[k], i), below.astype(BF16))
        put(k, 0, i, jnp.where(first, 0.0, above))
        put(k, top[k], i, jnp.where(last, 0.0, below))

    def pair(k, p, i):
        own = (lambda y: mid[y, i]) if k == 1 else (lambda y: center(k, y + 1, i))
        upper = edge[k][0, i] if p == 0 else own(p - 1)
        lower = edge[k][1, i] if p == rows[k] else own(p)
        return jnp.concatenate([upper, lower], 0)

    def folded(value):
        part = value.reshape(-1, 8, chans)
        return jnp.sum(part, 0), jnp.sum(part * part, 0)

    def conv_rows(k, apart):
        groups = [[i] for i in range(images)] if apart else [list(range(images))]
        sums = []
        for group in groups:
            bands = [
                jnp.concatenate([big[k][y + a, i] for i in group for y in range(rows[k])], 0)
                for a in range(3)
            ]
            total = mm(jnp.concatenate(bands, 1), smooth[k])
            total = total.reshape(len(group), rows[k], cols[k], chans)
            for j, i in enumerate(group):
                conv[k][i] = total[j]
                sums.append(folded(total[j]))
        return sums

    def conv_pairs(k, some, taps=(0, 1, 2), add=False, keep_sums=True):
        at = [slice(a * chans, (a + 1) * chans) for a in taps]
        weights = [
            jnp.concatenate([tap(k, a, 0) for a in taps], 0),
            jnp.concatenate([mixed[k, 0, here] for here in at], 0),
            jnp.concatenate([mixed[k, 1, here] for here in at], 0),
            jnp.concatenate([tap(k, a, 2) for a in taps], 0),
        ]
        parts = []
        for t in range(4):
            bands = [
                jnp.concatenate([vee[k][y + a, t, i] for y in some for i in range(images)], 0)
                for a in taps
            ]
            parts.append(mm(jnp.concatenate(bands, 1), weights[t]))
        even = (parts[1] + parts[2]) + parts[0]
        odd = (parts[1] - parts[2]) - parts[3]
        sums = [None] * images
        for j, (y, i) in enumerate((y, i) for y in some for i in range(images)):
            here = slice(j * half[k], (j + 1) * half[k])
            values = []
            for odd_ones, value in ((0, even[here]), (1, odd[here])):
                spots = [
                    conv[k].at[i, y, b, pl.ds(odd_ones, half[k], stride=2), :]
                    for b in range(blocks)
                ]
                if add:
                    value = value + jnp.concatenate([spot[...] for spot in spots], 1)
                for b, spot in enumerate(spots):
                    spot[...] = value[:, b * LANES : (b + 1) * LANES]
                values.append(value)
            if keep_sums:
                new = joined([[folded(value)] for value in values])[0]
                sums[i] = new if sums[i] is None else joined([[sums[i]], [new]])[0]
        return sums

    def joined(parts):
        total = parts[0]
        for part in parts[1:]:
            total = [(t[0] + u[0], t[1] + u[1]) for t, u in zip(total, part)]
        return total

    def stat_rows(sums):
        return [jnp.sum(part, 0, keepdims=True) for pair in sums for part in pair]

    def post(box, rows_of, send_sem, recv_sem):
        for j in range(box.shape[1]):
            some = rows_of[j * size : (j + 1) * size]
            some = some + [jnp.zeros_like(some[0])] * (size - len(some))
            box[0, j] = packed(some, size)
        for d in range(1, n):
            remote(box.at[0], box.at[d], send_sem.at[0], recv_sem.at[0], d).start()

    def all_of(box, sem):
        pltpu.make_async_copy(box.at[1:n], box.at[1:n], sem.at[0]).wait()

    def gathered(box):
        stats = []
        for j in range(box.shape[1]):
            total = box[0, j]
            for d in range(1, n):
                total = total + box[d, j]
            stats.append(unpacked(total, size))
        return jnp.concatenate(stats, 0)

    for i in range(images):
        for y in range(rows[3]):
            put(3, y + 1, i, five[i, y])
    halo_wait(3)
    for i in range(images):
        borders(3, i, recvs[3][0, i].astype(F32), recvs[3][1, i].astype(F32))

    outer = {}
    for p in range(rows[3] + 1):
        for i in range(images):
            both = mm(ups[2][...], pair(3, p, i))
            for y, value in ((2 * p - 1, both[: cols[2]]), (2 * p, both[cols[2] :])):
                if 0 <= y < rows[2]:
                    put(2, y + 1, i, lats[2][y, i] + value)
                else:
                    outer[y, i] = value
    carry_start(0)
    halo_wait(2)
    for i in range(images):
        borders(
            2,
            i,
            recvs[2][0, i].astype(F32) + outer[-1, i],
            recvs[2][1, i].astype(F32) + outer[rows[2], i],
        )

    def merge(k, p):
        for i in range(images):
            both = mm(ups[k][...], pair(k + 1, p, i))
            for y, value in ((2 * p - 1, both[: cols[k]]), (2 * p, both[cols[k] :])):
                if not 0 <= y < rows[k]:
                    hang[k][0 if y < 0 else 1, i] = value
                    continue
                even, odd = columns(k, y + 1 if k == 0 else y, i)
                even = even + value[: half[k]]
                odd = odd + value[half[k] :]
                if k:
                    mid[y, i, : half[k]] = even.astype(BF16)
                    mid[y, i, half[k] :] = odd.astype(BF16)
                put_pairs(k, y + 1, i, even, odd)

    def outside(k, way, i, even, odd):
        none = last if way else first
        put_pairs(
            k, way * top[k], i, jnp.where(none, 0.0, even), jnp.where(none, 0.0, odd)
        )

    for p in range(1, rows[2]):
        merge(1, p)
    sums_five = conv_rows(3, False)
    merge(1, 0)
    merge(1, rows[2])
    merge(0, 1)
    sums_four = conv_rows(2, True)
    sums_three = [conv_pairs(1, list(range(1, rows[1] - 1)))]
    merged, sums_two = 1, []

    def conv_two_row(y):
        nonlocal merged
        while merged < min((y + 2) // 2, rows[1] - 1):
            merged += 1
            merge(0, merged)
        sums_two.append(conv_pairs(0, [y]))

    inner = list(range(2, rows[0] - 2))
    for y in inner[: len(inner) // 2]:
        conv_two_row(y)

    carry_start(1)
    halo_wait(1)
    for way in range(2):
        for i in range(images):
            value = recvs[1][way, i].astype(F32) + hang[1][way, i]
            none = last if way else first
            own = mid[way * (rows[1] - 1), i]
            edge[1][way, i] = jnp.where(none, own, value.astype(BF16))
            outside(1, way, i, value[: half[1]], value[half[1] :])
    merge(0, 0)
    merge(0, rows[1])
    for y in inner[len(inner) // 2 :]:
        conv_two_row(y)
    sums_three.append(conv_pairs(1, [0, rows[1] - 1]))
    conv_two_row(1)
    conv_two_row(rows[0] - 2)
    conv_pairs(0, [0], (1, 2), keep_sums=False)
    conv_pairs(0, [rows[0] - 1], (0, 1), keep_sums=False)
    rest_rows = stat_rows(joined(sums_three)) + stat_rows(sums_four) + stat_rows(sums_five)
    post(box_rest, rest_rows, rest_send, rest_recv)

    halo_wait(0)
    for way in range(2):
        value = bias[0:1, :] + mm(recvs[0][way].reshape(images * cols[0], -1), lat_w[0][...])
        for i in range(images):
            keep(0, way * top[0], i, value[i * cols[0] : (i + 1) * cols[0]])
    for way in range(2):
        for i in range(images):
            even, odd = columns(0, way * top[0], i)
            even = even + hang[0][way, i, : half[0]]
            odd = odd + hang[0][way, i, half[0] :]
            outside(0, way, i, even, odd)
    sums_two.append(conv_pairs(0, [0], (0,), add=True))
    sums_two.append(conv_pairs(0, [rows[0] - 1], (2,), add=True))
    post(box_two, stat_rows(joined(sums_two)), two_send, two_recv)

    def scales(k, total, square):
        share = 1.0 / float(rows[k] * n * cols[k] * size)
        mean = total * share
        variance = square * share - mean * mean
        scale = lax.rsqrt(variance + EPSILON) * gain[k : k + 1, :]
        return scale, shift[k : k + 1, :] - mean * scale

    all_of(box_rest, rest_recv)
    rest = gathered(box_rest)
    for k in (1, 2, 3):
        for i in range(images):
            slot = ((k - 1) * images + i) * 2
            scale, offset = scales(k, rest[slot : slot + 1], rest[slot + 1 : slot + 2])
            if k == 1:
                for y in range(rows[k]):
                    value = jnp.concatenate([conv[k][i, y, b] for b in range(blocks)], 1)
                    done[k][i, y] = (value * scale + offset).astype(BF16)
            else:
                done[k][i] = (conv[k][i] * scale + offset).astype(BF16)
    on_ends(lambda way: [halo_copy(k, way).wait_send() for k in range(4)])
    carry(lambda way: pltpu.make_async_copy(hop, hop, hop_send.at[0]).wait())
    all_of(box_rest, rest_send)

    all_of(box_two, two_recv)
    two = gathered(box_two)
    for i in range(images):
        scale, offset = scales(0, two[2 * i : 2 * i + 1], two[2 * i + 1 : 2 * i + 2])
        affine[2 * i : 2 * i + 1, :] = scale
        affine[2 * i + 1 : 2 * i + 2, :] = offset
    all_of(box_two, two_send)


def finish_kernel(geom, *refs):
    images, rows = geom["images"], geom["rows"]
    conv_two, affine = refs[0:2]
    done = [None, *refs[2:5]]
    out_hbm, staged, rest_sem, two_sem = refs[5:9], refs[9], refs[10], refs[11]
    copies = []
    for k in (1, 2, 3):
        copies.append(pltpu.make_async_copy(done[k], out_hbm[k], rest_sem.at[k]))
        copies[-1].start()
    for i in range(images):
        scale = affine[2 * i : 2 * i + 1, :]
        offset = affine[2 * i + 1 : 2 * i + 2, :]
        for y in range(rows[0]):
            value = jnp.concatenate(
                [conv_two[i, y, b] for b in range(conv_two.shape[2])], 1
            )
            staged[i, y] = (value * scale + offset).astype(BF16)
            pltpu.make_async_copy(
                staged.at[i, y], out_hbm[0].at[i, y], two_sem.at[0]
            ).start()
    for copy in copies:
        copy.wait()
    pltpu.make_async_copy(staged, out_hbm[0], two_sem.at[0]).wait()


def per_device(n, *args):
    feats, lat_ws = args[0:4], args[4:8]
    bias, smooth, gain, shift = args[8:12]
    smooth = smooth.reshape(smooth.shape[0], -1, smooth.shape[3])
    images, chans = feats[0].shape[0], lat_ws[0].shape[1]
    rows = [f.shape[1] for f in feats]
    cols = [f.shape[2] for f in feats]
    geom = {"images": images, "chans": chans, "rows": rows, "cols": cols}
    any_spec = pl.BlockSpec(memory_space=pltpu.HBM)
    vmem_spec = pl.BlockSpec(memory_space=pltpu.VMEM)
    outs = [jax.ShapeDtypeStruct((images, r, c, chans), BF16) for r, c in zip(rows, cols)]
    dma = pltpu.SemaphoreType.DMA
    blocks = chans // LANES
    two_rows = -(-(images * 2) // 8) * 8
    strip = lambda k, count, width, kind: pltpu.VMEM((count, images, cols[k], width), kind)
    scratch = (
        [pltpu.VMEM(f.shape, BF16) for f in feats]
        + [pltpu.VMEM(w.shape, BF16) for w in lat_ws]
        + [pltpu.VMEM((3, *bias.shape), F32), pltpu.VMEM(smooth.shape, BF16)]
        + [pltpu.VMEM((2, 2, 3 * chans, chans), BF16)]
        + [pltpu.VMEM((rows[k] + 2, 4, images, cols[k] // 2, chans), BF16) for k in range(2)]
        + [strip(k, rows[k] + 2, 3 * chans, BF16) for k in (2, 3)]
        + [strip(k, min(rows[k], 2), chans, BF16) for k in range(1, 4)]
        + [strip(k, 2, chans, BF16) for k in range(4)]
        + [pltpu.VMEM((rows[0] + 2, images, blocks, cols[0], LANES), F32)]
        + [pltpu.VMEM((rows[1], images, blocks, cols[1], LANES), F32)]
        + [strip(2, rows[2], chans, F32)]
        + [pltpu.VMEM((images, rows[1], blocks, cols[1], LANES), F32)]
        + [pltpu.VMEM(o.shape, F32) for o in outs[2:]]
        + [pltpu.VMEM((2 * c, c), BF16) for c in cols[:3]]
        + [strip(k, 2, chans, BF16) for k in range(1, 4)]
        + [strip(k, 2, chans, F32) for k in range(2)]
        + [strip(1, rows[1], chans, BF16)]
        + [pltpu.VMEM((images, cols[0], chans), BF16)]
        + [
            pltpu.VMEM((n, -(-levels * images * 2 // (chans // GROUPS)), 1, chans), F32)
            for levels in (1, 3)
        ]
        + [dma((4,)), dma((4,)), dma((2,)), dma((1,))]
        + [dma((4, 2)), dma((4, 2)), dma((1,)), dma((2,))]
        + [dma((1,)) for _ in range(4)]
    )
    held = pl.pallas_call(
        functools.partial(kernel, n, geom),
        out_shape=[pltpu.VMEM((images, rows[0], blocks, cols[0], LANES), F32)]
        + [pltpu.VMEM(o.shape, BF16) for o in outs[1:]]
        + [pltpu.VMEM((two_rows, chans), F32)],
        in_specs=[any_spec] * 12,
        out_specs=[vmem_spec] * 5,
        scratch_shapes=scratch,
        compiler_params=pltpu.CompilerParams(
            collective_id=0, has_side_effects=True, vmem_limit_bytes=KERNEL_BYTES
        ),
    )(*args[:8], bias, gain, shift, smooth)
    held = [pltpu.with_memory_space_constraint(h, pltpu.VMEM) for h in held]
    return pl.pallas_call(
        functools.partial(finish_kernel, geom),
        out_shape=outs,
        in_specs=[vmem_spec] * 5,
        out_specs=[any_spec] * 4,
        scratch_shapes=[pltpu.VMEM(outs[0].shape, BF16), dma((4,)), dma((1,))],
        compiler_params=pltpu.CompilerParams(vmem_limit_bytes=16 * 1024 * 1024),
    )(held[0], held[4], *held[1:4])


def solution(mesh):
    strips = P("batch", "rows", None, None)
    run = functools.partial(per_device, mesh.shape["rows"])
    return jax.shard_map(
        lambda *args: tuple(run(*args)),
        mesh=mesh,
        in_specs=(strips,) * 4 + (P(),) * 8,
        out_specs=(strips,) * 4,
        check_vma=False,
    )
```

time: 23.4 us -> 21.8 us (0.932)
  Pallas kernels: 22.6 us -> 21 us
    pallas_call x1, Pallas kernels: 21 us -> 19.4 us  [per_device(): pl.pallas_call(functools.partial(kernel, n, geom), out_shape=[pltpu.VMEM(...]
where the time goes in v3:
time: 21.8 us; the launch traced here: 21.7 us
  Pallas kernels  21 us (96%)
  between operations  0.64 us (3%)
    pallas_call x1, Pallas kernels, per_device(): pl.pallas_call(functools.partial(kernel, n, geom), out_shape=[pltpu.VMEM(...  19.4 us
    pallas_call x1, Pallas kernels, per_device(): pl.pallas_call(functools.partial(finish_kernel, geom), out_shape=outs, in...  1.59 us

profile of v3, /device:TPU:0, one launch (start us, length us, event | category | flops | bytes accessed | tf_op | source)
XLA Modules:
  0.0 21.7 jit_solution(15140829772590388710)
XLA Ops:
  0.6 19.4 %shard_map.147 = (f32[2,8,2,256,128]{4,3,2,1,0:T(8,128)S(1)}, bf16[2,4,128,256]{3,2,1,0:T(8,128)(2,1)S(1)}, bf16[2,2,64,256]{3,2,1,0:T(8,128)(2,1)S(1)}, bf16[2,1,32,256]{3,2,1,0:T(8,128)(2,1)S(1)}, f32[8,256]{1,0:T(8,128)S(1)}) custom-call(bf16[2,8,256,256]{3,2,1,0:T(8,128)(2,1)} %refs_0_.1, bf16[2,4,128,512]{3,2,1,0:T(8,128)(2,1)} %refs_1_.1, ...), custom_call_target="tpu_custom_call" | custom-call | tf_op jit(solution)/shard_map/pallas_call | solution.py:652
  20.1 1.6 %shard_map.148 = (bf16[2,8,256,256]{3,2,1,0:T(8,128)(2,1)}, bf16[2,4,128,256]{3,2,1,0:T(8,128)(2,1)}, bf16[2,2,64,256]{3,2,1,0:T(8,128)(2,1)}, bf16[2,1,32,256]{3,2,1,0:T(8,128)(2,1)}) custom-call(f32[2,8,2,256,128]{4,3,2,1,0:T(8,128)S(1)} %get-tuple-element.9.refs_0_, f32[8,256]{1,0:T(8,128)S(1)} %get-tuple-element.10.refs_1_, ...), custom_call_target="tpu_custom_call" | custom-call | tf_op jit(solution)/shard_map/pallas_call | solution.py:665

commit v4 on v3

--- a/solution.py
+++ b/solution.py
@@ -40,11 +40,6 @@
 
 def mm(a, b):
     return jnp.dot(a, b, preferred_element_type=F32)
-
-
-def mm_halves(start, a, b, step):
-    cut = -(-(a.shape[1] // step) // 2) * step
-    return (start + mm(a[:, :cut], b[:cut])) + mm(a[:, cut:], b[cut:])
 
 
 def group_totals(value, size):
@@ -135,6 +130,14 @@
     for copy in smooth_copy:
         copy.start()
 
+    @pl.when(first)
+    def _():
+        recvs[0][0] = jnp.zeros_like(recvs[0][0])
+
+    @pl.when(last)
+    def _():
+        recvs[0][1] = jnp.zeros_like(recvs[0][1])
+
     for k in range(3):
         odd, even = bilinear(cols[k], k < 2, k == 0)
         ups[k][0 : cols[k]] = odd
@@ -241,11 +244,13 @@
     pltpu.make_async_copy(consts, consts, p_sem.at[0]).wait()
     feat_copy[3].wait()
     lat_copy[3].wait()
-    flat = feat[3][...].reshape(-1, feat[3].shape[-1])
-    five = mm_halves(bias[3:4, :], flat, lat_w[3], chans)
-    five = five.reshape(images, rows[3], cols[3], chans)
+    five = []
+    for i in range(images):
+        flat = feat[3][i].reshape(rows[3] * cols[3], -1)
+        five.append((bias[3:4, :] + mm(flat, lat_w[3][...])).reshape(rows[3], cols[3], chans))
     for y in range(rows[3]):
-        sends[3][y] = five[:, y].astype(BF16)
+        for i in range(images):
+            sends[3][y, i] = five[i][y].astype(BF16)
     pl.semaphore_wait(barrier, n - 1)
     halo_start(3)
 
@@ -448,7 +453,7 @@
 
     for i in range(images):
         for y in range(rows[3]):
-            put(3, y + 1, i, five[i, y])
+            put(3, y + 1, i, five[i][y])
     halo_wait(3)
     for i in range(images):
         borders(3, i, recvs[3][0, i].astype(F32), recvs[3][1, i].astype(F32))
@@ -462,21 +467,13 @@
                     put(2, y + 1, i, lats[2][y, i] + value)
                 else:
                     outer[y, i] = value
-    carry_start(0)
-    halo_wait(2)
-    for i in range(images):
-        borders(
-            2,
-            i,
-            recvs[2][0, i].astype(F32) + outer[-1, i],
-            recvs[2][1, i].astype(F32) + outer[rows[2], i],
-        )
-
     def merge(k, p):
         for i in range(images):
             both = mm(ups[k][...], pair(k + 1, p, i))
             for y, value in ((2 * p - 1, both[: cols[k]]), (2 * p, both[cols[k] :])):
                 if not 0 <= y < rows[k]:
+                    if k == 0:
+                        value = jnp.where(first if y < 0 else last, 0.0, value + bias[0:1, :])
                     hang[k][0 if y < 0 else 1, i] = value
                     continue
                 even, odd = columns(k, y + 1 if k == 0 else y, i)
@@ -487,33 +484,37 @@
                     mid[y, i, half[k] :] = odd.astype(BF16)
                 put_pairs(k, y + 1, i, even, odd)
 
-    def outside(k, way, i, even, odd):
-        none = last if way else first
-        put_pairs(
-            k, way * top[k], i, jnp.where(none, 0.0, even), jnp.where(none, 0.0, odd)
-        )
-
+    sums_five = conv_rows(3, False)
     for p in range(1, rows[2]):
         merge(1, p)
-    sums_five = conv_rows(3, False)
+    for p in range(2, rows[1] - 1):
+        merge(0, p)
+
+    halo_wait(2)
+    for i in range(images):
+        borders(
+            2,
+            i,
+            recvs[2][0, i].astype(F32) + outer[-1, i],
+            recvs[2][1, i].astype(F32) + outer[rows[2], i],
+        )
+
     merge(1, 0)
     merge(1, rows[2])
     merge(0, 1)
+    merge(0, rows[1] - 1)
     sums_four = conv_rows(2, True)
     sums_three = [conv_pairs(1, list(range(1, rows[1] - 1)))]
-    merged, sums_two = 1, []
+    sums_two = []
 
     def conv_two_row(y):
-        nonlocal merged
-        while merged < min((y + 2) // 2, rows[1] - 1):
-            merged += 1
-            merge(0, merged)
         sums_two.append(conv_pairs(0, [y]))
 
     inner = list(range(2, rows[0] - 2))
     for y in inner[: len(inner) // 2]:
         conv_two_row(y)
 
+    carry_start(0)
     carry_start(1)
     halo_wait(1)
     for way in range(2):
@@ -522,7 +523,8 @@
             none = last if way else first
             own = mid[way * (rows[1] - 1), i]
             edge[1][way, i] = jnp.where(none, own, value.astype(BF16))
-            outside(1, way, i, value[: half[1]], value[half[1] :])
+            value = jnp.where(none, 0.0, value)
+            put_pairs(1, way * top[1], i, value[: half[1]], value[half[1] :])
     merge(0, 0)
     merge(0, rows[1])
     for y in inner[len(inner) // 2 :]:
@@ -537,7 +539,7 @@
 
     halo_wait(0)
     for way in range(2):
-        value = bias[0:1, :] + mm(recvs[0][way].reshape(images * cols[0], -1), lat_w[0][...])
+        value = mm(recvs[0][way].reshape(images * cols[0], -1), lat_w[0][...])
         for i in range(images):
             keep(0, way * top[0], i, value[i * cols[0] : (i + 1) * cols[0]])
     for way in range(2):
@@ -545,7 +547,7 @@
             even, odd = columns(0, way * top[0], i)
             even = even + hang[0][way, i, : half[0]]
             odd = odd + hang[0][way, i, half[0] :]
-            outside(0, way, i, even, odd)
+            put_pairs(0, way * top[0], i, even, odd)
     sums_two.append(conv_pairs(0, [0], (0,), add=True))
     sums_two.append(conv_pairs(0, [rows[0] - 1], (2,), add=True))
     post(box_two, stat_rows(joined(sums_two)), two_send, two_recv)

time: 21.8 us -> 21.3 us (0.977)
  Pallas kernels: 21 us -> 20.5 us
    pallas_call x1, Pallas kernels: 19.4 us -> 18.9 us  [per_device(): pl.pallas_call(functools.partial(kernel, n, geom), out_shape=[pltpu.VMEM(...]
where the time goes in v4:
time: 21.3 us; the launch traced here: 21.1 us
  Pallas kernels  20.5 us (96%)
  between operations  0.64 us (3%)
    pallas_call x1, Pallas kernels, per_device(): pl.pallas_call(functools.partial(kernel, n, geom), out_shape=[pltpu.VMEM(...  18.9 us
    pallas_call x1, Pallas kernels, per_device(): pl.pallas_call(functools.partial(finish_kernel, geom), out_shape=outs, in...  1.59 us

profile of v4, /device:TPU:0, one launch (start us, length us, event | category | flops | bytes accessed | tf_op | source)
XLA Modules:
  0.0 21.1 jit_solution(14849122037214440109)
XLA Ops:
  0.6 18.9 %shard_map.147 = (f32[2,8,2,256,128]{4,3,2,1,0:T(8,128)S(1)}, bf16[2,4,128,256]{3,2,1,0:T(8,128)(2,1)S(1)}, bf16[2,2,64,256]{3,2,1,0:T(8,128)(2,1)S(1)}, bf16[2,1,32,256]{3,2,1,0:T(8,128)(2,1)S(1)}, f32[8,256]{1,0:T(8,128)S(1)}) custom-call(bf16[2,8,256,256]{3,2,1,0:T(8,128)(2,1)} %refs_0_.1, bf16[2,4,128,512]{3,2,1,0:T(8,128)(2,1)} %refs_1_.1, ...), custom_call_target="tpu_custom_call" | custom-call | tf_op jit(solution)/shard_map/pallas_call | solution.py:654
  19.5 1.6 %shard_map.148 = (bf16[2,8,256,256]{3,2,1,0:T(8,128)(2,1)}, bf16[2,4,128,256]{3,2,1,0:T(8,128)(2,1)}, bf16[2,2,64,256]{3,2,1,0:T(8,128)(2,1)}, bf16[2,1,32,256]{3,2,1,0:T(8,128)(2,1)}) custom-call(f32[2,8,2,256,128]{4,3,2,1,0:T(8,128)S(1)} %get-tuple-element.9.refs_0_, f32[8,256]{1,0:T(8,128)S(1)} %get-tuple-element.10.refs_1_, ...), custom_call_target="tpu_custom_call" | custom-call | tf_op jit(solution)/shard_map/pallas_call | solution.py:667

commit v5 on v4

--- a/solution.py
+++ b/solution.py
@@ -184,7 +184,12 @@
 
     span = 2 * max(1, math.isqrt(n // 2))
     early = images // 2
-    pieces = ((0, early), (early, images)) if early else ((0, images), (0, images))
+    later = slice(early, images)
+    pieces = (
+        (slice(0, early), slice(0, cols[0])),
+        (later, slice(0, half[0])),
+        (later, slice(half[0], cols[0])),
+    )
     place = lax.rem(me, span)
     crosses = (
         jnp.logical_and(place == 0, jnp.logical_not(first)),
@@ -209,37 +214,39 @@
 
             @pl.when(crosses[way])
             def _():
-                for j in hops:
-                    here = slice(*pieces[j])
+                for j in (*hops, 2):
+                    some, width = pieces[j]
+                    last_hop = j == 2
                     remote(
-                        feat[0].at[here, way * (rows[0] - 1)],
-                        hop.at[here],
+                        feat[0].at[some, way * (rows[0] - 1), width],
+                        recvs[0].at[1 - way, some, width] if last_hop else hop.at[some, width],
                         halo_send.at[0, way],
-                        hop_recv.at[j],
-                        span if way else -span,
+                        halo_recv.at[0, 1 - way] if last_hop else hop_recv.at[j],
+                        (1 if last_hop else span) * (1 if way else -1),
                     ).start()
 
         on_ends(begin)
 
-    def carry(act):
+    def carry(act, ways=(0, 1)):
         if relays:
-            for way in range(2):
+            for way in ways:
                 pl.when(carries[way])(functools.partial(act, way))
 
-    def carry_start(j):
+    def carry_start(j, *ways):
         def act(way):
-            here = hop.at[slice(*pieces[j])]
+            some, width = pieces[j]
+            here = hop.at[some, width]
             pltpu.make_async_copy(here, here, hop_recv.at[j]).wait()
             remote(
                 here,
-                recvs[0].at[1 - way, slice(*pieces[j])],
-                hop_send.at[0],
+                recvs[0].at[1 - way, some, width],
+                hop_send.at[j],
                 halo_recv.at[0, 1 - way],
                 1 - span if way else span - 1,
             ).start()
 
         if j in hops:
-            carry(act)
+            carry(act, ways)
 
     pltpu.make_async_copy(consts, consts, p_sem.at[0]).wait()
     feat_copy[3].wait()
@@ -469,8 +476,9 @@
                     outer[y, i] = value
     def merge(k, p):
         for i in range(images):
-            both = mm(ups[k][...], pair(k + 1, p, i))
-            for y, value in ((2 * p - 1, both[: cols[k]]), (2 * p, both[cols[k] :])):
+            coarse = pair(k + 1, p, i)
+            for y in (2 * p - 1, 2 * p):
+                value = mm(ups[k][: cols[k]] if y < 2 * p else ups[k][cols[k] :], coarse)
                 if not 0 <= y < rows[k]:
                     if k == 0:
                         value = jnp.where(first if y < 0 else last, 0.0, value + bias[0:1, :])
@@ -490,6 +498,7 @@
     for p in range(2, rows[1] - 1):
         merge(0, p)
 
+    carry_start(0, 1)
     halo_wait(2)
     for i in range(images):
         borders(
@@ -511,11 +520,12 @@
         sums_two.append(conv_pairs(0, [y]))
 
     inner = list(range(2, rows[0] - 2))
-    for y in inner[: len(inner) // 2]:
+    ahead = len(inner) * 3 // 4
+    for y in inner[:ahead]:
         conv_two_row(y)
 
-    carry_start(0)
-    carry_start(1)
+    carry_start(0, 0)
+    carry_start(1, 0, 1)
     halo_wait(1)
     for way in range(2):
         for i in range(images):
@@ -527,9 +537,9 @@
             put_pairs(1, way * top[1], i, value[: half[1]], value[half[1] :])
     merge(0, 0)
     merge(0, rows[1])
-    for y in inner[len(inner) // 2 :]:
+    sums_three.append(conv_pairs(1, [0, rows[1] - 1]))
+    for y in inner[ahead:]:
         conv_two_row(y)
-    sums_three.append(conv_pairs(1, [0, rows[1] - 1]))
     conv_two_row(1)
     conv_two_row(rows[0] - 2)
     conv_pairs(0, [0], (1, 2), keep_sums=False)
@@ -539,9 +549,8 @@
 
     halo_wait(0)
     for way in range(2):
-        value = mm(recvs[0][way].reshape(images * cols[0], -1), lat_w[0][...])
-        for i in range(images):
-            keep(0, way * top[0], i, value[i * cols[0] : (i + 1) * cols[0]])
+        for i in range(images):
+            keep(0, way * top[0], i, mm(recvs[0][way, i], lat_w[0][...]))
     for way in range(2):
         for i in range(images):
             even, odd = columns(0, way * top[0], i)
@@ -560,11 +569,11 @@
         return scale, shift[k : k + 1, :] - mean * scale
 
     all_of(box_rest, rest_recv)
-    rest = gathered(box_rest)
+    coarse = gathered(box_rest)
     for k in (1, 2, 3):
         for i in range(images):
             slot = ((k - 1) * images + i) * 2
-            scale, offset = scales(k, rest[slot : slot + 1], rest[slot + 1 : slot + 2])
+            scale, offset = scales(k, coarse[slot : slot + 1], coarse[slot + 1 : slot + 2])
             if k == 1:
                 for y in range(rows[k]):
                     value = jnp.concatenate([conv[k][i, y, b] for b in range(blocks)], 1)
@@ -572,7 +581,9 @@
             else:
                 done[k][i] = (conv[k][i] * scale + offset).astype(BF16)
     on_ends(lambda way: [halo_copy(k, way).wait_send() for k in range(4)])
-    carry(lambda way: pltpu.make_async_copy(hop, hop, hop_send.at[0]).wait())
+    for j in hops:
+        here = hop.at[pieces[j]]
+        carry(lambda way, h=here, j=j: pltpu.make_async_copy(h, h, hop_send.at[j]).wait())
     all_of(box_rest, rest_send)
 
     all_of(box_two, two_recv)
@@ -648,7 +659,7 @@
             for levels in (1, 3)
         ]
         + [dma((4,)), dma((4,)), dma((2,)), dma((1,))]
-        + [dma((4, 2)), dma((4, 2)), dma((1,)), dma((2,))]
+        + [dma((4, 2)), dma((4, 2)), dma((2,)), dma((2,))]
         + [dma((1,)) for _ in range(4)]
     )
     held = pl.pallas_call(

time: 21.3 us -> 20.7 us (0.972)
  Pallas kernels: 20.5 us -> 19.9 us
    pallas_call x1, Pallas kernels: 18.9 us -> 18.3 us  [per_device(): pl.pallas_call(functools.partial(kernel, n, geom), out_shape=[pltpu.VMEM(...]
where the time goes in v5:
time: 20.7 us; the launch traced here: 20.6 us
  Pallas kernels  19.9 us (96%)
  between operations  0.64 us (3%)
    pallas_call x1, Pallas kernels, per_device(): pl.pallas_call(functools.partial(kernel, n, geom), out_shape=[pltpu.VMEM(...  18.3 us
    pallas_call x1, Pallas kernels, per_device(): pl.pallas_call(functools.partial(finish_kernel, geom), out_shape=outs, in...  1.59 us

profile of v5, /device:TPU:0, one launch (start us, length us, event | category | flops | bytes accessed | tf_op | source)
XLA Modules:
  0.0 20.6 jit_solution(9961948502976717422)
XLA Ops:
  0.6 18.3 %shard_map.147 = (f32[2,8,2,256,128]{4,3,2,1,0:T(8,128)S(1)}, bf16[2,4,128,256]{3,2,1,0:T(8,128)(2,1)S(1)}, bf16[2,2,64,256]{3,2,1,0:T(8,128)(2,1)S(1)}, bf16[2,1,32,256]{3,2,1,0:T(8,128)(2,1)S(1)}, f32[8,256]{1,0:T(8,128)S(1)}) custom-call(bf16[2,8,256,256]{3,2,1,0:T(8,128)(2,1)} %refs_0_.1, bf16[2,4,128,512]{3,2,1,0:T(8,128)(2,1)} %refs_1_.1, ...), custom_call_target="tpu_custom_call" | custom-call | tf_op jit(solution)/shard_map/pallas_call | solution.py:665
  19.0 1.6 %shard_map.148 = (bf16[2,8,256,256]{3,2,1,0:T(8,128)(2,1)}, bf16[2,4,128,256]{3,2,1,0:T(8,128)(2,1)}, bf16[2,2,64,256]{3,2,1,0:T(8,128)(2,1)}, bf16[2,1,32,256]{3,2,1,0:T(8,128)(2,1)}) custom-call(f32[2,8,2,256,128]{4,3,2,1,0:T(8,128)S(1)} %get-tuple-element.9.refs_0_, f32[8,256]{1,0:T(8,128)S(1)} %get-tuple-element.10.refs_1_, ...), custom_call_target="tpu_custom_call" | custom-call | tf_op jit(solution)/shard_map/pallas_call | solution.py:678

commit v6 on v5

--- a/solution.py
+++ b/solution.py
@@ -251,13 +251,15 @@
     pltpu.make_async_copy(consts, consts, p_sem.at[0]).wait()
     feat_copy[3].wait()
     lat_copy[3].wait()
-    five = []
-    for i in range(images):
-        flat = feat[3][i].reshape(rows[3] * cols[3], -1)
-        five.append((bias[3:4, :] + mm(flat, lat_w[3][...])).reshape(rows[3], cols[3], chans))
+    flat = feat[3][...].reshape(-1, feat[3].shape[-1])
+    five = [
+        mm(flat, lat_w[3][:, b * LANES : (b + 1) * LANES]) for b in range(blocks)
+    ]
+    five = bias[3:4, :] + jnp.concatenate(five, 1)
+    five = five.reshape(images, rows[3], cols[3], chans)
     for y in range(rows[3]):
         for i in range(images):
-            sends[3][y, i] = five[i][y].astype(BF16)
+            sends[3][y, i] = five[i, y].astype(BF16)
     pl.semaphore_wait(barrier, n - 1)
     halo_start(3)
 
@@ -460,7 +462,7 @@
 
     for i in range(images):
         for y in range(rows[3]):
-            put(3, y + 1, i, five[i][y])
+            put(3, y + 1, i, five[i, y])
     halo_wait(3)
     for i in range(images):
         borders(3, i, recvs[3][0, i].astype(F32), recvs[3][1, i].astype(F32))
@@ -510,9 +512,8 @@
 
     merge(1, 0)
     merge(1, rows[2])
+    sums_four = conv_rows(2, True)
     merge(0, 1)
-    merge(0, rows[1] - 1)
-    sums_four = conv_rows(2, True)
     sums_three = [conv_pairs(1, list(range(1, rows[1] - 1)))]
     sums_two = []
 
@@ -522,6 +523,8 @@
     inner = list(range(2, rows[0] - 2))
     ahead = len(inner) * 3 // 4
     for y in inner[:ahead]:
+        if y == inner[min(2, ahead - 1)]:
+            merge(0, rows[1] - 1)
         conv_two_row(y)
 
     carry_start(0, 0)

time: 20.7 us -> 20.7 us (level)
  no operation moved by 1% of the time
where the time goes in v6:
time: 20.7 us; the launch traced here: 20.6 us
  Pallas kernels  19.9 us (96%)
  between operations  0.64 us (3%)
    pallas_call x1, Pallas kernels, per_device(): pl.pallas_call(functools.partial(kernel, n, geom), out_shape=[pltpu.VMEM(...  18.3 us
    pallas_call x1, Pallas kernels, per_device(): pl.pallas_call(functools.partial(finish_kernel, geom), out_shape=outs, in...  1.59 us

profile of v6, /device:TPU:0, one launch (start us, length us, event | category | flops | bytes accessed | tf_op | source)
XLA Modules:
  0.0 20.6 jit_solution(7642357108717180839)
XLA Ops:
  0.6 18.3 %shard_map.147 = (f32[2,8,2,256,128]{4,3,2,1,0:T(8,128)S(1)}, bf16[2,4,128,256]{3,2,1,0:T(8,128)(2,1)S(1)}, bf16[2,2,64,256]{3,2,1,0:T(8,128)(2,1)S(1)}, bf16[2,1,32,256]{3,2,1,0:T(8,128)(2,1)S(1)}, f32[8,256]{1,0:T(8,128)S(1)}) custom-call(bf16[2,8,256,256]{3,2,1,0:T(8,128)(2,1)} %refs_0_.1, bf16[2,4,128,512]{3,2,1,0:T(8,128)(2,1)} %refs_1_.1, ...), custom_call_target="tpu_custom_call" | custom-call | tf_op jit(solution)/shard_map/pallas_call | solution.py:668
  19.0 1.6 %shard_map.148 = (bf16[2,8,256,256]{3,2,1,0:T(8,128)(2,1)}, bf16[2,4,128,256]{3,2,1,0:T(8,128)(2,1)}, bf16[2,2,64,256]{3,2,1,0:T(8,128)(2,1)}, bf16[2,1,32,256]{3,2,1,0:T(8,128)(2,1)}) custom-call(f32[2,8,2,256,128]{4,3,2,1,0:T(8,128)S(1)} %get-tuple-element.9.refs_0_, f32[8,256]{1,0:T(8,128)S(1)} %get-tuple-element.10.refs_1_, ...), custom_call_target="tpu_custom_call" | custom-call | tf_op jit(solution)/shard_map/pallas_call | solution.py:681

commit v7 on v6

--- a/solution.py
+++ b/solution.py
@@ -86,19 +86,18 @@
     feat_hbm, lat_hbm = take(4), take(4)
     consts_hbm, smooth_hbm = take(3), take(1)[0]
     (conv_two,) = take(1)
-    done = [None] + take(3)
+    conv = [conv_two] + take(3)
     (affine,) = take(1)
     feat, lat_w = take(4), take(4)
     consts, smooth, mixed = take(3)
     vee, big = take(2), [None, None] + take(2)
     sends, recvs, lats = [None] + take(3), take(4), take(3)
-    conv = [conv_two] + take(3)
     ups, edge, hang = take(3), [None] + take(3), take(2)
     mid, hop = take(2)
-    box_two, box_rest = take(2)
+    (box,) = take(1)
     in_sem, w_sem, s_sem, p_sem = take(4)
     halo_send, halo_recv, hop_send, hop_recv = take(4)
-    two_send, two_recv, rest_send, rest_recv = take(4)
+    sum_send, sum_recv = take(2)
     bias, gain, shift = (consts.at[j] for j in range(3))
 
     me = lax.axis_index("rows")
@@ -547,8 +546,7 @@
     conv_two_row(rows[0] - 2)
     conv_pairs(0, [0], (1, 2), keep_sums=False)
     conv_pairs(0, [rows[0] - 1], (0, 1), keep_sums=False)
-    rest_rows = stat_rows(joined(sums_three)) + stat_rows(sums_four) + stat_rows(sums_five)
-    post(box_rest, rest_rows, rest_send, rest_recv)
+    coarse_rows = stat_rows(joined(sums_three)) + stat_rows(sums_four) + stat_rows(sums_five)
 
     halo_wait(0)
     for way in range(2):
@@ -562,7 +560,7 @@
             put_pairs(0, way * top[0], i, even, odd)
     sums_two.append(conv_pairs(0, [0], (0,), add=True))
     sums_two.append(conv_pairs(0, [rows[0] - 1], (2,), add=True))
-    post(box_two, stat_rows(joined(sums_two)), two_send, two_recv)
+    post(box, stat_rows(joined(sums_two)) + coarse_rows, sum_send, sum_recv)
 
     def scales(k, total, square):
         share = 1.0 / float(rows[k] * n * cols[k] * size)
@@ -571,56 +569,46 @@
         scale = lax.rsqrt(variance + EPSILON) * gain[k : k + 1, :]
         return scale, shift[k : k + 1, :] - mean * scale
 
-    all_of(box_rest, rest_recv)
-    coarse = gathered(box_rest)
-    for k in (1, 2, 3):
-        for i in range(images):
-            slot = ((k - 1) * images + i) * 2
-            scale, offset = scales(k, coarse[slot : slot + 1], coarse[slot + 1 : slot + 2])
-            if k == 1:
-                for y in range(rows[k]):
-                    value = jnp.concatenate([conv[k][i, y, b] for b in range(blocks)], 1)
-                    done[k][i, y] = (value * scale + offset).astype(BF16)
-            else:
-                done[k][i] = (conv[k][i] * scale + offset).astype(BF16)
     on_ends(lambda way: [halo_copy(k, way).wait_send() for k in range(4)])
     for j in hops:
         here = hop.at[pieces[j]]
         carry(lambda way, h=here, j=j: pltpu.make_async_copy(h, h, hop_send.at[j]).wait())
-    all_of(box_rest, rest_send)
-
-    all_of(box_two, two_recv)
-    two = gathered(box_two)
-    for i in range(images):
-        scale, offset = scales(0, two[2 * i : 2 * i + 1], two[2 * i + 1 : 2 * i + 2])
-        affine[2 * i : 2 * i + 1, :] = scale
-        affine[2 * i + 1 : 2 * i + 2, :] = offset
-    all_of(box_two, two_send)
+    all_of(box, sum_recv)
+    stats = gathered(box)
+    for k in range(4):
+        for i in range(images):
+            slot = (k * images + i) * 2
+            scale, offset = scales(k, stats[slot : slot + 1], stats[slot + 1 : slot + 2])
+            affine[slot : slot + 1, :] = scale
+            affine[slot + 1 : slot + 2, :] = offset
+    all_of(box, sum_send)
 
 
 def finish_kernel(geom, *refs):
     images, rows = geom["images"], geom["rows"]
-    conv_two, affine = refs[0:2]
-    done = [None, *refs[2:5]]
-    out_hbm, staged, rest_sem, two_sem = refs[5:9], refs[9], refs[10], refs[11]
-    copies = []
+    conv, affine = refs[0:4], refs[4]
+    out_hbm, staged, out_sem = refs[5:9], refs[9:13], refs[13]
+
+    def finish(k, i, y):
+        if k < 2:
+            value = jnp.concatenate([conv[k][i, y, b] for b in range(conv[k].shape[2])], 1)
+        else:
+            value = conv[k][i, y]
+        slot = (k * images + i) * 2
+        value = value * affine[slot : slot + 1, :] + affine[slot + 1 : slot + 2, :]
+        staged[k][i, y] = value.astype(BF16)
+
+    for i in range(images):
+        for y in range(rows[0]):
+            finish(0, i, y)
+            pltpu.make_async_copy(staged[0].at[i, y], out_hbm[0].at[i, y], out_sem.at[0]).start()
     for k in (1, 2, 3):
-        copies.append(pltpu.make_async_copy(done[k], out_hbm[k], rest_sem.at[k]))
-        copies[-1].start()
-    for i in range(images):
-        scale = affine[2 * i : 2 * i + 1, :]
-        offset = affine[2 * i + 1 : 2 * i + 2, :]
-        for y in range(rows[0]):
-            value = jnp.concatenate(
-                [conv_two[i, y, b] for b in range(conv_two.shape[2])], 1
-            )
-            staged[i, y] = (value * scale + offset).astype(BF16)
-            pltpu.make_async_copy(
-                staged.at[i, y], out_hbm[0].at[i, y], two_sem.at[0]
-            ).start()
-    for copy in copies:
-        copy.wait()
-    pltpu.make_async_copy(staged, out_hbm[0], two_sem.at[0]).wait()
+        for i in range(images):
+            for y in range(rows[k]):
+                finish(k, i, y)
+        pltpu.make_async_copy(staged[k], out_hbm[k], out_sem.at[k]).start()
+    for k in range(4):
+        pltpu.make_async_copy(staged[k], out_hbm[k], out_sem.at[k]).wait()
 
 
 def per_device(n, *args):
@@ -636,7 +624,7 @@
     outs = [jax.ShapeDtypeStruct((images, r, c, chans), BF16) for r, c in zip(rows, cols)]
     dma = pltpu.SemaphoreType.DMA
     blocks = chans // LANES
-    two_rows = -(-(images * 2) // 8) * 8
+    stat_rows = -(-(4 * images * 2) // 8) * 8
     strip = lambda k, count, width, kind: pltpu.VMEM((count, images, cols[k], width), kind)
     scratch = (
         [pltpu.VMEM(f.shape, BF16) for f in feats]
@@ -650,26 +638,25 @@
         + [pltpu.VMEM((rows[0] + 2, images, blocks, cols[0], LANES), F32)]
         + [pltpu.VMEM((rows[1], images, blocks, cols[1], LANES), F32)]
         + [strip(2, rows[2], chans, F32)]
-        + [pltpu.VMEM((images, rows[1], blocks, cols[1], LANES), F32)]
-        + [pltpu.VMEM(o.shape, F32) for o in outs[2:]]
         + [pltpu.VMEM((2 * c, c), BF16) for c in cols[:3]]
         + [strip(k, 2, chans, BF16) for k in range(1, 4)]
         + [strip(k, 2, chans, F32) for k in range(2)]
         + [strip(1, rows[1], chans, BF16)]
         + [pltpu.VMEM((images, cols[0], chans), BF16)]
         + [
-            pltpu.VMEM((n, -(-levels * images * 2 // (chans // GROUPS)), 1, chans), F32)
-            for levels in (1, 3)
+            pltpu.VMEM((n, -(-4 * images * 2 // (chans // GROUPS)), 1, chans), F32)
         ]
         + [dma((4,)), dma((4,)), dma((2,)), dma((1,))]
         + [dma((4, 2)), dma((4, 2)), dma((2,)), dma((2,))]
-        + [dma((1,)) for _ in range(4)]
+        + [dma((1,)) for _ in range(2)]
     )
     held = pl.pallas_call(
         functools.partial(kernel, n, geom),
-        out_shape=[pltpu.VMEM((images, rows[0], blocks, cols[0], LANES), F32)]
-        + [pltpu.VMEM(o.shape, BF16) for o in outs[1:]]
-        + [pltpu.VMEM((two_rows, chans), F32)],
+        out_shape=[
+            pltpu.VMEM((images, rows[k], blocks, cols[k], LANES), F32) for k in range(2)
+        ]
+        + [pltpu.VMEM(o.shape, F32) for o in outs[2:]]
+        + [pltpu.VMEM((stat_rows, chans), F32)],
         in_specs=[any_spec] * 12,
         out_specs=[vmem_spec] * 5,
         scratch_shapes=scratch,
@@ -683,9 +670,9 @@
         out_shape=outs,
         in_specs=[vmem_spec] * 5,
         out_specs=[any_spec] * 4,
-        scratch_shapes=[pltpu.VMEM(outs[0].shape, BF16), dma((4,)), dma((1,))],
+        scratch_shapes=[pltpu.VMEM(o.shape, BF16) for o in outs] + [dma((4,))],
         compiler_params=pltpu.CompilerParams(vmem_limit_bytes=16 * 1024 * 1024),
-    )(held[0], held[4], *held[1:4])
+    )(*held)
 
 
 def solution(mesh):

time: 20.7 us -> 20.7 us (level)
  no operation moved by 1% of the time
where the time goes in v7:
time: 20.7 us; the launch traced here: 20.6 us
  Pallas kernels  19.9 us (96%)
  between operations  0.64 us (3%)
    pallas_call x1, Pallas kernels, per_device(): pl.pallas_call(functools.partial(kernel, n, geom), out_shape=[pltpu.VMEM(...  18.4 us
    pallas_call x1, Pallas kernels, per_device(): pl.pallas_call(functools.partial(finish_kernel, geom), out_shape=outs, in...  1.58 us

profile of v7, /device:TPU:0, one launch (start us, length us, event | category | flops | bytes accessed | tf_op | source)
XLA Modules:
  0.0 20.6 jit_solution(15645580787947509413)
XLA Ops:
  0.6 18.4 %shard_map.147 = (f32[2,8,2,256,128]{4,3,2,1,0:T(8,128)S(1)}, f32[2,4,2,128,128]{4,3,2,1,0:T(8,128)S(1)}, f32[2,2,64,256]{3,2,1,0:T(8,128)S(1)}, f32[2,1,32,256]{3,2,1,0:T(8,128)S(1)}, f32[16,256]{1,0:T(8,128)S(1)}) custom-call(bf16[2,8,256,256]{3,2,1,0:T(8,128)(2,1)} %refs_0_.1, bf16[2,4,128,512]{3,2,1,0:T(8,128)(2,1)} %refs_1_.1, ...), custom_call_target="tpu_custom_call" | custom-call | tf_op jit(solution)/shard_map/pallas_call | solution.py:653
  19.0 1.6 %shard_map.148 = (bf16[2,8,256,256]{3,2,1,0:T(8,128)(2,1)}, bf16[2,4,128,256]{3,2,1,0:T(8,128)(2,1)}, bf16[2,2,64,256]{3,2,1,0:T(8,128)(2,1)}, bf16[2,1,32,256]{3,2,1,0:T(8,128)(2,1)}) custom-call(f32[2,8,2,256,128]{4,3,2,1,0:T(8,128)S(1)} %get-tuple-element.9.refs_0_, f32[2,4,2,128,128]{4,3,2,1,0:T(8,128)S(1)} %get-tuple-element.10.refs_1_, ...), custom_call_target="tpu_custom_call" | custom-call | tf_op jit(solution)/shard_map/pallas_call | solution.py:668

commit v8 on v6

--- a/solution.py
+++ b/solution.py
@@ -97,8 +97,9 @@
     mid, hop = take(2)
     box_two, box_rest = take(2)
     in_sem, w_sem, s_sem, p_sem = take(4)
-    halo_send, halo_recv, hop_send, hop_recv = take(4)
-    two_send, two_recv, rest_send, rest_recv = take(4)
+    halo_recv, hop_recv = take(2)
+    two_send, two_recv, rest_recv = take(3)
+    halo_send, hop_send, rest_send = (in_sem, w_sem), s_sem, p_sem
     bias, gain, shift = (consts.at[j] for j in range(3))
 
     me = lax.axis_index("rows")
@@ -162,7 +163,7 @@
         return remote(
             halo_source(k, way),
             recvs[k].at[1 - way],
-            halo_send.at[k, way],
+            halo_send[way].at[k],
             halo_recv.at[k, 1 - way],
             1 if way else -1,
         )
@@ -220,7 +221,7 @@
                     remote(
                         feat[0].at[some, way * (rows[0] - 1), width],
                         recvs[0].at[1 - way, some, width] if last_hop else hop.at[some, width],
-                        halo_send.at[0, way],
+                        halo_send[way].at[0],
                         halo_recv.at[0, 1 - way] if last_hop else hop_recv.at[j],
                         (1 if last_hop else span) * (1 if way else -1),
                     ).start()
@@ -662,8 +663,8 @@
             for levels in (1, 3)
         ]
         + [dma((4,)), dma((4,)), dma((2,)), dma((1,))]
-        + [dma((4, 2)), dma((4, 2)), dma((2,)), dma((2,))]
-        + [dma((1,)) for _ in range(4)]
+        + [dma((4, 2)), dma((2,))]
+        + [dma((1,)) for _ in range(3)]
     )
     held = pl.pallas_call(
         functools.partial(kernel, n, geom),

time: 20.7 us -> 20.6 us (level)
  no operation moved by 1% of the time
where the time goes in v8:
time: 20.6 us; the launch traced here: 20.5 us
  Pallas kernels  19.8 us (96%)
  between operations  0.64 us (3%)
    pallas_call x1, Pallas kernels, per_device(): pl.pallas_call(functools.partial(kernel, n, geom), out_shape=[pltpu.VMEM(...  18.2 us
    pallas_call x1, Pallas kernels, per_device(): pl.pallas_call(functools.partial(finish_kernel, geom), out_shape=outs, in...  1.59 us

profile of v8, /device:TPU:0, one launch (start us, length us, event | category | flops | bytes accessed | tf_op | source)
XLA Modules:
  0.0 20.5 jit_solution(5710329879263271853)
XLA Ops:
  0.6 18.2 %shard_map.147 = (f32[2,8,2,256,128]{4,3,2,1,0:T(8,128)S(1)}, bf16[2,4,128,256]{3,2,1,0:T(8,128)(2,1)S(1)}, bf16[2,2,64,256]{3,2,1,0:T(8,128)(2,1)S(1)}, bf16[2,1,32,256]{3,2,1,0:T(8,128)(2,1)S(1)}, f32[8,256]{1,0:T(8,128)S(1)}) custom-call(bf16[2,8,256,256]{3,2,1,0:T(8,128)(2,1)} %refs_0_.1, bf16[2,4,128,512]{3,2,1,0:T(8,128)(2,1)} %refs_1_.1, ...), custom_call_target="tpu_custom_call" | custom-call | tf_op jit(solution)/shard_map/pallas_call | solution.py:669
  18.9 1.6 %shard_map.148 = (bf16[2,8,256,256]{3,2,1,0:T(8,128)(2,1)}, bf16[2,4,128,256]{3,2,1,0:T(8,128)(2,1)}, bf16[2,2,64,256]{3,2,1,0:T(8,128)(2,1)}, bf16[2,1,32,256]{3,2,1,0:T(8,128)(2,1)}) custom-call(f32[2,8,2,256,128]{4,3,2,1,0:T(8,128)S(1)} %get-tuple-element.9.refs_0_, f32[8,256]{1,0:T(8,128)S(1)} %get-tuple-element.10.refs_1_, ...), custom_call_target="tpu_custom_call" | custom-call | tf_op jit(solution)/shard_map/pallas_call | solution.py:682
